TPU v7x, 256 devices: a 4x2x16 block of a 4x16x16 slice. The times are simulated.
256 devices in a mesh: grp: 2 (over y), row: 64 (over x, z), col: 2 (over core).
Axes of the slice: x: 4, y: 2, z: 16, core: 2. Of those that a mesh axis runs over, the one named last changes fastest.
The devices are a block of a 4x16x16 slice.
Arguments:
- queries: bfloat16 [65536, 2, 128], P(('grp', 'row', 'col')), parts along dimension 0, may hold values from -6 to 6
- keys: bfloat16 [65536, 2, 128], P(('grp', 'row', 'col')), parts along dimension 0, may hold values from -6 to 6
- values: bfloat16 [65536, 2, 128], P(('grp', 'row', 'col')), parts along dimension 0, may hold values from -6 to 6
Outputs:
- attended: bfloat16 [65536, 256], P(('grp', 'row', 'col')), parts along dimension 0
There are 2 independent parts, one for each index of `grp`. A program takes and returns all parts, laid end to end along the dimension named above; each array names one. Nothing has to cross between parts.
All inputs are finite; a program needn't handle non-finite values.
Results may differ from a plain program's by a relative error of at most 0.014.
Values may be sent and summed in bfloat16 or wider, within the bound.
No kernel may reach another device: no remote copies, remote signals or barrier semaphores. Data moves between devices by JAX's collectives and lax.ppermute only.
A program may use at most 128 MiB of HBM per device.

v0:
```python
import math

import jax
import jax.numpy as jnp
from jax import lax
from jax.sharding import PartitionSpec as P


def laid_out(pieces, dim):
    pieces = jnp.moveaxis(pieces, 0, dim)
    lengths = pieces.shape
    return pieces.reshape(*lengths[:dim], lengths[dim] * lengths[dim + 1], *lengths[dim + 2 :])


def copy_for_each(value, axis):
    devices = lax.axis_size(axis)
    return lax.all_to_all(
        jnp.broadcast_to(value[None], (devices, *value.shape)), axis, 0, 0, tiled=True
    )


def gather_directly(value, axis, dim):
    return laid_out(copy_for_each(value, axis), dim)


def side_by_side(arrays, axis, dim, along):
    widths = [a.shape[along] for a in arrays]
    both = jnp.concatenate(arrays, axis=along)
    result = lax.all_gather(both, axis, axis=dim, tiled=True)
    return tuple(jnp.split(result, [sum(widths[:k]) for k in range(1, len(widths))], axis=along))


def split_up(value, dim, devices):
    before, after = (value.shape[:dim], value.shape[dim + 1 :])
    return jnp.moveaxis(value.reshape(*before, devices, -1, *after), dim, 0)


def summed_on_arrival(value, axis, dim):
    devices = lax.axis_size(axis)
    pieces = lax.all_to_all(split_up(value, dim, devices), axis, 0, 0, tiled=True)
    return jnp.sum(pieces.astype(jnp.float32), axis=0)


def side_by_side_2(arrays, axis, dim, along):
    columns = [a.reshape(*a.shape[:along], -1) for a in arrays]
    both = jnp.concatenate(columns, axis=along)
    result, at, finished = (summed_on_arrival(both, axis, dim), 0, [])
    for a, column in zip(arrays, columns):
        share = result[..., at : at + column.shape[along]]
        finished.append(share.reshape(*share.shape[:along], *a.shape[along:]))
        at += column.shape[along]
    return tuple(finished)


def attend(running, portion, offset, query_rows, widest=2048):
    key_rows, value_rows = portion
    length_rows = key_rows.shape[0]
    span_rows = math.gcd(length_rows, widest)
    scale = query_rows.shape[-1] ** (-0.5)
    key_blocks = key_rows.reshape(
        length_rows // span_rows, span_rows, key_rows.shape[1], key_rows.shape[2]
    )
    value_blocks = value_rows.reshape(
        length_rows // span_rows, span_rows, value_rows.shape[1], value_rows.shape[2]
    )

    def advance(carried, blocks):
        highest, summed, accum = carried
        key_block, value_block = blocks
        scores = (
            jnp.einsum("qhd,khd->hqk", query_rows, key_block, preferred_element_type=jnp.float32)
            * scale
        )
        raised = jnp.maximum(highest, jnp.max(scores, axis=-1))
        factor = jnp.exp(highest - raised)
        weights = jnp.exp(scores - raised[..., None]).astype(jnp.bfloat16)
        summed = summed * factor + jnp.sum(weights.astype(jnp.float32), axis=-1)
        accum = accum * factor[..., None] + jnp.einsum(
            "hqk,khd->hqd", weights, value_block, preferred_element_type=jnp.float32
        )
        return ((raised, summed, accum), None)

    running, _ = lax.scan(advance, running, (key_blocks, value_blocks))
    return running


def starting(heads, n_rows, width):
    return (
        jnp.full((heads, n_rows), -1e30, jnp.float32),
        jnp.zeros((heads, n_rows), jnp.float32),
        jnp.zeros((heads, n_rows, width), jnp.float32),
    )


def body(queries, keys, values):
    own_rows = queries.shape[0]
    heads = queries.shape[1]
    width = queries.shape[2]
    query_rows = gather_directly(queries, "col", 0)
    n_rows = query_rows.shape[0]
    folded = attend(
        starting(heads, n_rows, width),
        side_by_side((keys, values), "row", 0, 1),
        jnp.int32(0),
        query_rows=query_rows,
    )
    peak, summed, accum = folded
    highest = lax.pmax(peak, "col")
    factor = jnp.exp(peak - highest)
    accum, summed = side_by_side_2(
        ((accum * factor[..., None]).astype(jnp.bfloat16), (summed * factor).astype(jnp.bfloat16)),
        "col",
        1,
        2,
    )
    result = accum / summed[..., None]
    output = jnp.transpose(result, (1, 0, 2)).reshape(own_rows, heads * width)
    return output.astype(jnp.bfloat16)


def solution(mesh):
    placed = (
        P(("grp", "row", "col"), None, None),
        P(("grp", "row", "col"), None, None),
        P(("grp", "row", "col"), None, None),
    )
    return jax.shard_map(
        body, mesh=mesh, in_specs=placed, out_specs=P(("grp", "row", "col"), None), check_vma=False
    )
```

profile of v0, /device:TPU:33, one launch (start us, length us, event | category | flops | bytes accessed | tf_op | source)
XLA Modules:
  0.0 360.2 jit_solution(8800663758129540582)
XLA Ops:
  10.8 23.9 %all-to-all-start = ((bf16[2,256,2,128]{3,1,2,0:T(8,128)(2,1)}), bf16[2,256,2,128]{3,1,2,0:T(8,128)(2,1)S(1)}, u32[]{:S(2)}, u32[]{:S(2)}) async-start(bf16[2,256,2,128]{3,1,2,0:T(8,128)(2,1)} %broadcast_in_dim.21), calls=%async_computation | async-start | bytes 524288 | tf_op jit(solution)/shard_map/all_to_all | solution.py:17
  35.9 177.1 %all-gather.2.cloned.1.call-done = bf16[16384,4,128]{2,0,1:T(8,128)(2,1)} async-done(((bf16[256,4,128]{2,0,1:T(8,128)(2,1)}), bf16[16384,4,128]{2,0,1:T(8,128)(2,1)}) %all-gather.2.cloned.1.call-update) | async-done | bytes 16777232 | tf_op jit(solution)/shard_map/all_gather | solution.py:29
  213.1 11.3 %fusion.14 = (bf16[16384,2,128]{2,0,1:T(8,128)(2,1)}, bf16[16384,2,128]{2,0,1:T(8,128)(2,1)}) fusion(bf16[16384,4,128]{2,0,1:T(8,128)(2,1)} %all-gather.2.cloned.1.call-done), kind=kLoop, calls=%fused_computation.29 | loop fusion | bytes 33554432 | tf_op jit(solution)/shard_map/split | solution.py:30
  224.3 118.7 %while.15 = (s32[]{:T(128)}, f32[2,512]{1,0:T(2,128)S(1)}, f32[2,512]{1,0:T(2,128)S(1)}, f32[2,512,128]{2,1,0:T(8,128)S(1)}, bf16[8,2048,2,128]{3,1,0,2:T(8,128)...) while((s32[]{:T(128)}, f32[2,512]{1,0:T(2,128)S(1)}, ...), condition=%wide.region_3.4_spmd.clone, body=%wide.region_0.3_spmd.clone.sunk | while | flops 1095111680 | bytes 62194820 | solution.py:83
  224.3 5.7 %bitcast_reduce_fusion.2 = (f32[2,512]{1,0:T(2,128)S(1)}, f32[2,2048,512]{2,1,0:T(8,128)}) fusion(bf16[512,2,128]{2,0,1:T(8,128)(2,1)S(1)} %get-tuple-element.195, bf16[8,2048,2,128]{3,1,0,2:T(8,128)(2,1)} %get-tuple-element.194, s32[]{:T(128)} %get-tuple-element.181), kind=kOutput, calls=%fused_computation.1.clone.1 | convolution fusion | flops 541064192 | bytes 9703936 | tf_op jit(solution)/shard_map/while/body/eval_jaxpr/qhd,khd->hqk/dot_general | solution.py:71
  230.0 4.9 %convert_reduce_fusion.3 = f32[2,512]{1,0:T(2,128)S(1)} fusion(f32[2,512]{1,0:T(2,128)S(1)} %fusion.24, f32[2,2048,512]{2,1,0:T(8,128)} %get-tuple-element.169), kind=kLoop, calls=%fused_computation.4.clone.1 | loop fusion | flops 10484736 | bytes 8396800 | tf_op jit(solution)/shard_map/while/body/eval_jaxpr/reduce_sum | solution.py:77
  235.8 3.3 convolution_add_fusion.2
  239.2 5.7 %bitcast_reduce_fusion.2 = (f32[2,512]{1,0:T(2,128)S(1)}, f32[2,2048,512]{2,1,0:T(8,128)}) fusion(bf16[512,2,128]{2,0,1:T(8,128)(2,1)S(1)} %get-tuple-element.195, bf16[8,2048,2,128]{3,1,0,2:T(8,128)(2,1)} %get-tuple-element.194, s32[]{:T(128)} %get-tuple-element.181), kind=kOutput, calls=%fused_computation.1.clone.1 | convolution fusion | flops 541064192 | bytes 9703936 | tf_op jit(solution)/shard_map/while/body/eval_jaxpr/qhd,khd->hqk/dot_general | solution.py:71
  244.9 4.9 %convert_reduce_fusion.3 = f32[2,512]{1,0:T(2,128)S(1)} fusion(f32[2,512]{1,0:T(2,128)S(1)} %fusion.24, f32[2,2048,512]{2,1,0:T(8,128)} %get-tuple-element.169), kind=kLoop, calls=%fused_computation.4.clone.1 | loop fusion | flops 10484736 | bytes 8396800 | tf_op jit(solution)/shard_map/while/body/eval_jaxpr/reduce_sum | solution.py:77
  250.7 3.3 convolution_add_fusion.2
  254.0 5.7 %bitcast_reduce_fusion.2 = (f32[2,512]{1,0:T(2,128)S(1)}, f32[2,2048,512]{2,1,0:T(8,128)}) fusion(bf16[512,2,128]{2,0,1:T(8,128)(2,1)S(1)} %get-tuple-element.195, bf16[8,2048,2,128]{3,1,0,2:T(8,128)(2,1)} %get-tuple-element.194, s32[]{:T(128)} %get-tuple-element.181), kind=kOutput, calls=%fused_computation.1.clone.1 | convolution fusion | flops 541064192 | bytes 9703936 | tf_op jit(solution)/shard_map/while/body/eval_jaxpr/qhd,khd->hqk/dot_general | solution.py:71
  259.7 4.9 %convert_reduce_fusion.3 = f32[2,512]{1,0:T(2,128)S(1)} fusion(f32[2,512]{1,0:T(2,128)S(1)} %fusion.24, f32[2,2048,512]{2,1,0:T(8,128)} %get-tuple-element.169), kind=kLoop, calls=%fused_computation.4.clone.1 | loop fusion | flops 10484736 | bytes 8396800 | tf_op jit(solution)/shard_map/while/body/eval_jaxpr/reduce_sum | solution.py:77
  268.9 5.7 %bitcast_reduce_fusion.2 = (f32[2,512]{1,0:T(2,128)S(1)}, f32[2,2048,512]{2,1,0:T(8,128)}) fusion(bf16[512,2,128]{2,0,1:T(8,128)(2,1)S(1)} %get-tuple-element.195, bf16[8,2048,2,128]{3,1,0,2:T(8,128)(2,1)} %get-tuple-element.194, s32[]{:T(128)} %get-tuple-element.181), kind=kOutput, calls=%fused_computation.1.clone.1 | convolution fusion | flops 541064192 | bytes 9703936 | tf_op jit(solution)/shard_map/while/body/eval_jaxpr/qhd,khd->hqk/dot_general | solution.py:71
  274.6 4.9 %convert_reduce_fusion.3 = f32[2,512]{1,0:T(2,128)S(1)} fusion(f32[2,512]{1,0:T(2,128)S(1)} %fusion.24, f32[2,2048,512]{2,1,0:T(8,128)} %get-tuple-element.169), kind=kLoop, calls=%fused_computation.4.clone.1 | loop fusion | flops 10484736 | bytes 8396800 | tf_op jit(solution)/shard_map/while/body/eval_jaxpr/reduce_sum | solution.py:77
  283.7 5.7 %bitcast_reduce_fusion.2 = (f32[2,512]{1,0:T(2,128)S(1)}, f32[2,2048,512]{2,1,0:T(8,128)}) fusion(bf16[512,2,128]{2,0,1:T(8,128)(2,1)S(1)} %get-tuple-element.195, bf16[8,2048,2,128]{3,1,0,2:T(8,128)(2,1)} %get-tuple-element.194, s32[]{:T(128)} %get-tuple-element.181), kind=kOutput, calls=%fused_computation.1.clone.1 | convolution fusion | flops 541064192 | bytes 9703936 | tf_op jit(solution)/shard_map/while/body/eval_jaxpr/qhd,khd->hqk/dot_general | solution.py:71
  289.4 4.9 %convert_reduce_fusion.3 = f32[2,512]{1,0:T(2,128)S(1)} fusion(f32[2,512]{1,0:T(2,128)S(1)} %fusion.24, f32[2,2048,512]{2,1,0:T(8,128)} %get-tuple-element.169), kind=kLoop, calls=%fused_computation.4.clone.1 | loop fusion | flops 10484736 | bytes 8396800 | tf_op jit(solution)/shard_map/while/body/eval_jaxpr/reduce_sum | solution.py:77
  298.6 5.7 %bitcast_reduce_fusion.2 = (f32[2,512]{1,0:T(2,128)S(1)}, f32[2,2048,512]{2,1,0:T(8,128)}) fusion(bf16[512,2,128]{2,0,1:T(8,128)(2,1)S(1)} %get-tuple-element.195, bf16[8,2048,2,128]{3,1,0,2:T(8,128)(2,1)} %get-tuple-element.194, s32[]{:T(128)} %get-tuple-element.181), kind=kOutput, calls=%fused_computation.1.clone.1 | convolution fusion | flops 541064192 | bytes 9703936 | tf_op jit(solution)/shard_map/while/body/eval_jaxpr/qhd,khd->hqk/dot_general | solution.py:71
  304.3 4.9 %convert_reduce_fusion.3 = f32[2,512]{1,0:T(2,128)S(1)} fusion(f32[2,512]{1,0:T(2,128)S(1)} %fusion.24, f32[2,2048,512]{2,1,0:T(8,128)} %get-tuple-element.169), kind=kLoop, calls=%fused_computation.4.clone.1 | loop fusion | flops 10484736 | bytes 8396800 | tf_op jit(solution)/shard_map/while/body/eval_jaxpr/reduce_sum | solution.py:77
  313.4 5.7 %bitcast_reduce_fusion.2 = (f32[2,512]{1,0:T(2,128)S(1)}, f32[2,2048,512]{2,1,0:T(8,128)}) fusion(bf16[512,2,128]{2,0,1:T(8,128)(2,1)S(1)} %get-tuple-element.195, bf16[8,2048,2,128]{3,1,0,2:T(8,128)(2,1)} %get-tuple-element.194, s32[]{:T(128)} %get-tuple-element.181), kind=kOutput, calls=%fused_computation.1.clone.1 | convolution fusion | flops 541064192 | bytes 9703936 | tf_op jit(solution)/shard_map/while/body/eval_jaxpr/qhd,khd->hqk/dot_general | solution.py:71
  319.1 4.9 %convert_reduce_fusion.3 = f32[2,512]{1,0:T(2,128)S(1)} fusion(f32[2,512]{1,0:T(2,128)S(1)} %fusion.24, f32[2,2048,512]{2,1,0:T(8,128)} %get-tuple-element.169), kind=kLoop, calls=%fused_computation.4.clone.1 | loop fusion | flops 10484736 | bytes 8396800 | tf_op jit(solution)/shard_map/while/body/eval_jaxpr/reduce_sum | solution.py:77
  328.3 5.7 %bitcast_reduce_fusion.2 = (f32[2,512]{1,0:T(2,128)S(1)}, f32[2,2048,512]{2,1,0:T(8,128)}) fusion(bf16[512,2,128]{2,0,1:T(8,128)(2,1)S(1)} %get-tuple-element.195, bf16[8,2048,2,128]{3,1,0,2:T(8,128)(2,1)} %get-tuple-element.194, s32[]{:T(128)} %get-tuple-element.181), kind=kOutput, calls=%fused_computation.1.clone.1 | convolution fusion | flops 541064192 | bytes 9703936 | tf_op jit(solution)/shard_map/while/body/eval_jaxpr/qhd,khd->hqk/dot_general | solution.py:71
  334.0 4.9 %convert_reduce_fusion.3 = f32[2,512]{1,0:T(2,128)S(1)} fusion(f32[2,512]{1,0:T(2,128)S(1)} %fusion.24, f32[2,2048,512]{2,1,0:T(8,128)} %get-tuple-element.169), kind=kLoop, calls=%fused_computation.4.clone.1 | loop fusion | flops 10484736 | bytes 8396800 | tf_op jit(solution)/shard_map/while/body/eval_jaxpr/reduce_sum | solution.py:77
  343.1 3.6 pmax.7
  347.9 3.9 %all_to_all.10 = bf16[2,2,256,129]{2,1,3,0:T(2,128)(2,1)S(1)} all-to-all(bf16[2,2,256,129]{2,1,3,0:T(2,128)(2,1)S(1)} %copy.41), channel_id=1, replica_groups=mesh['grp'=2,'row'=64,'col'=2] {'col'}, dimensions={0} | all-to-all | bytes 528384 | tf_op jit(solution)/shard_map/all_to_all | solution.py:40
  (70 shorter events, 35.0 us)
Async XLA Ops:
  6.5 206.5 %all-gather.2.cloned.1.call-start = ((), (), s32[]{:S(2)}) async-start(), calls=%async_computation.2 | async-start | bytes 17039360 | tf_op jit(solution)/shard_map/all_gather | solution.py:29
  10.8 25.1 %all-to-all-start = ((bf16[2,256,2,128]{3,1,2,0:T(8,128)(2,1)}), bf16[2,256,2,128]{3,1,2,0:T(8,128)(2,1)S(1)}, u32[]{:S(2)}, u32[]{:S(2)}) async-start(bf16[2,256,2,128]{3,1,2,0:T(8,128)(2,1)} %broadcast_in_dim.21), calls=%async_computation | async-start | bytes 524288 | tf_op jit(solution)/shard_map/all_to_all | solution.py:17
  230.0 5.8 %copy-start = (f32[2,2048,512]{2,1,0:T(8,128)S(1)}, f32[2,2048,512]{2,1,0:T(8,128)}, u32[]{:S(2)}) copy-start(f32[2,2048,512]{2,1,0:T(8,128)} %get-tuple-element.169) | copy-start | bytes 25165828 | tf_op jit(solution)/shard_map/while
  244.9 5.8 %copy-start = (f32[2,2048,512]{2,1,0:T(8,128)S(1)}, f32[2,2048,512]{2,1,0:T(8,128)}, u32[]{:S(2)}) copy-start(f32[2,2048,512]{2,1,0:T(8,128)} %get-tuple-element.169) | copy-start | bytes 25165828 | tf_op jit(solution)/shard_map/while
  259.7 5.8 %copy-start = (f32[2,2048,512]{2,1,0:T(8,128)S(1)}, f32[2,2048,512]{2,1,0:T(8,128)}, u32[]{:S(2)}) copy-start(f32[2,2048,512]{2,1,0:T(8,128)} %get-tuple-element.169) | copy-start | bytes 25165828 | tf_op jit(solution)/shard_map/while
  274.6 5.8 %copy-start = (f32[2,2048,512]{2,1,0:T(8,128)S(1)}, f32[2,2048,512]{2,1,0:T(8,128)}, u32[]{:S(2)}) copy-start(f32[2,2048,512]{2,1,0:T(8,128)} %get-tuple-element.169) | copy-start | bytes 25165828 | tf_op jit(solution)/shard_map/while
  289.4 5.8 %copy-start = (f32[2,2048,512]{2,1,0:T(8,128)S(1)}, f32[2,2048,512]{2,1,0:T(8,128)}, u32[]{:S(2)}) copy-start(f32[2,2048,512]{2,1,0:T(8,128)} %get-tuple-element.169) | copy-start | bytes 25165828 | tf_op jit(solution)/shard_map/while
  304.3 5.8 %copy-start = (f32[2,2048,512]{2,1,0:T(8,128)S(1)}, f32[2,2048,512]{2,1,0:T(8,128)}, u32[]{:S(2)}) copy-start(f32[2,2048,512]{2,1,0:T(8,128)} %get-tuple-element.169) | copy-start | bytes 25165828 | tf_op jit(solution)/shard_map/while
  319.1 5.8 %copy-start = (f32[2,2048,512]{2,1,0:T(8,128)S(1)}, f32[2,2048,512]{2,1,0:T(8,128)}, u32[]{:S(2)}) copy-start(f32[2,2048,512]{2,1,0:T(8,128)} %get-tuple-element.169) | copy-start | bytes 25165828 | tf_op jit(solution)/shard_map/while
  334.0 5.8 %copy-start = (f32[2,2048,512]{2,1,0:T(8,128)S(1)}, f32[2,2048,512]{2,1,0:T(8,128)}, u32[]{:S(2)}) copy-start(f32[2,2048,512]{2,1,0:T(8,128)} %get-tuple-element.169) | copy-start | bytes 25165828 | tf_op jit(solution)/shard_map/while
Sparse Core Ops, SparseCore 0:
  9.8 203.2 all-gather.1
where the time goes:
time: 361 us; the launch traced here: 360 us
  waiting for transfers between devices  178 us (49%)
  matrix products  72.4 us (20%)
  other arithmetic  41 us (11%)
  starting transfers between devices  23.9 us (7%)
  local copies, waits for them, and re-layouts  23.3 us (6%)
  between operations  13.5 us (4%)
  blocking collectives  7.53 us (2%)
    all_gather x1, waiting for transfers between devices, side_by_side(): result = lax.all_gather(both, axis, axis=dim, tiled=True)  177 us
    dot_general x8, matrix products, advance(): jnp.einsum('qhd,khd->hqk', query_rows, key_block, preferred_element_type=...  45.6 us
    reduce_sum x8, other arithmetic, advance(): summed = summed * factor + jnp.sum(weights.astype(jnp.float32), axis=-1)  39.3 us
    dot_general x8, matrix products, advance(): jnp.einsum('hqk,khd->hqd', weights, value_block, preferred_element_type=j...  26.7 us
    all_to_all x1, starting transfers between devices, copy_for_each(): lax.all_to_all(jnp.broadcast_to(value[None], (devices, *value.shape)), ax...  23.9 us
    split x1, local copies, waits for them, and re-layouts, side_by_side(): jnp.split(result, [sum(widths[:k]) for k in range(1, len(widths))], axis=...  11.3 us
  transfers between devices with their start and end apart: 2, of which 2 were waited for; matrix products, arithmetic and copies ran while one was open for 0% of the time, Pallas kernels for 0%

commit v1 on v0

v1 whole, which is shorter than its diff:
```python
import functools
import math

import jax
import jax.numpy as jnp
from jax import lax
from jax.experimental import pallas as pl
from jax.experimental.pallas import tpu as pltpu
from jax.sharding import Mesh
from jax.sharding import PartitionSpec as P


ROW_X = 4
BLOCK = 512
STAT_ROWS = 16
VMEM = pl.BlockSpec(memory_space=pltpu.VMEM)
SMEM = pl.BlockSpec(memory_space=pltpu.SMEM)
NT = (((1,), (1,)), ((), ()))


def fold_kernel(*refs, pieces, heads, width, block, first):
    kv_refs, q_ref = refs[:pieces], refs[pieces]
    if first:
        acc_out, stat_out, v_turned, score = refs[pieces + 1 :]
    else:
        acc_in, stat_in, acc_out, stat_out, v_turned, score = refs[pieces + 1 :]
    rows = kv_refs[0].shape[0] // 2
    scale = width ** (-0.5) * math.log2(math.e)
    n_blocks = acc_out.shape[2] // block
    for h in range(heads):
        lanes = slice(h * width, (h + 1) * width)
        for i in range(pieces):
            v_turned[h, :, i * rows : (i + 1) * rows] = kv_refs[i][rows:, lanes].T

    def span(j):
        return pl.ds(pl.multiple_of(j * block, block), block)

    def score_of(h, j):
        lanes = slice(h * width, (h + 1) * width)
        q = q_ref[h, span(j), :]
        for i in range(pieces):
            s = lax.dot_general(kv_refs[i][:rows, lanes], q, NT, preferred_element_type=jnp.float32)
            score[h, i * rows : (i + 1) * rows, :] = s * scale

    def finish(h, j):
        at = span(j)
        s = score[h]
        top = s.max(axis=0, keepdims=True)
        if not first:
            top = jnp.maximum(top, stat_in[h, 0:1, at])
        p = jnp.exp2(s - top)
        total = p.sum(axis=0, keepdims=True)
        mixed = jnp.dot(v_turned[h], p.astype(jnp.bfloat16), preferred_element_type=jnp.float32)
        if not first:
            fade = jnp.exp2(stat_in[h, 0:1, at] - top)
            total = total + stat_in[h, 1:2, at] * fade
            mixed = mixed + acc_in[h, :, at] * fade
        acc_out[h, :, at] = mixed
        stat_out[h, 0:1, at] = top
        stat_out[h, 1:2, at] = total

    score_of(0, 0)

    def step(j, _):
        for h in range(heads):
            if h + 1 < heads:
                score_of(h + 1, j)
            else:
                score_of(0, jnp.minimum(j + 1, n_blocks - 1))
            finish(h, j)
        return 0

    lax.fori_loop(0, n_blocks, step, 0)


def fold(state, chunks, queries, count=None):
    pieces, rows = len(chunks), chunks[0].shape[0] // 2
    heads, everyone, width = queries.shape
    count = everyone if count is None else count
    first = state is None
    operands = [*chunks, queries, *(() if first else state)]
    aliases = {} if first or count < everyone else {pieces + 1: 0, pieces + 2: 1}
    flops = 4 * heads * width * count * rows * pieces
    return pl.pallas_call(
        functools.partial(
            fold_kernel, pieces=pieces, heads=heads, width=width, block=BLOCK, first=first
        ),
        out_shape=(
            jax.ShapeDtypeStruct((heads, width, count), jnp.float32),
            jax.ShapeDtypeStruct((heads, 8, count), jnp.float32),
        ),
        in_specs=[VMEM] * len(operands),
        out_specs=(VMEM, VMEM),
        scratch_shapes=[
            pltpu.VMEM((heads, width, pieces * rows), jnp.bfloat16),
            pltpu.VMEM((heads, pieces * rows, BLOCK), jnp.float32),
        ],
        input_output_aliases=aliases,
        compiler_params=pltpu.CompilerParams(vmem_limit_bytes=8 * 2**20),
        cost_estimate=pl.CostEstimate(
            flops=flops, transcendentals=heads * count * rows * pieces, bytes_accessed=0
        ),
        name="fold",
    )(*operands)


def lay_kernel(*refs, heads, width):
    pieces, out_ref = refs[:-1], refs[-1]
    rows = pieces[0].shape[0]
    for at, part in enumerate(pieces):
        for h in range(heads):
            out_ref[h, at * rows : (at + 1) * rows, :] = part[:, h * width : (h + 1) * width]


def lay(pieces, heads):
    rows, lanes = pieces[0].shape
    width = lanes // heads
    return pl.pallas_call(
        functools.partial(lay_kernel, heads=heads, width=width),
        out_shape=jax.ShapeDtypeStruct((heads, len(pieces) * rows, width), pieces[0].dtype),
        in_specs=[VMEM] * len(pieces),
        out_specs=VMEM,
        compiler_params=pltpu.CompilerParams(vmem_limit_bytes=4 * 2**20),
        name="lay",
    )(*pieces)


def log_weight(stats, h):
    at = 3 * h
    return stats[at : at + 1] + stats[at + 1 : at + 2] + stats[at + 2 : at + 3]


def pack_kernel(dest_ref, acc_ref, stat_ref, *refs, heads, width, own, start):
    (more_ref, out_ref) = refs if len(refs) == 2 else (None, refs[0])
    owners = out_ref.shape[0]
    count = owners * own
    at = slice(start, start + count)
    which = lax.broadcasted_iota(jnp.int32, (STAT_ROWS, count), 0)
    stats = jnp.zeros((STAT_ROWS, count), jnp.float32)
    scales = []
    for h in range(heads):
        top, total = stat_ref[h, 0:1, at], stat_ref[h, 1:2, at]
        fade = share = None
        if more_ref is not None:
            log = jnp.concatenate(
                [log_weight(more_ref[j, heads * width :, :].astype(jnp.float32), h) for j in range(owners)],
                axis=1,
            )
            raised = jnp.maximum(top, log)
            fade, share = jnp.exp2(top - raised), jnp.exp2(log - raised)
            total, top = total * fade + share, raised
        weight = 1.0 / total
        scales.append((weight, None) if fade is None else (fade * weight, share * weight))
        rest = top + jnp.log2(total)
        for part in range(3):
            rounded = rest.astype(jnp.bfloat16).astype(jnp.float32)
            stats = jnp.where(which == 3 * h + part, rounded, stats)
            rest = rest - rounded
    stats = stats.astype(jnp.bfloat16)
    for j in range(owners):
        to, here = dest_ref[j], slice(j * own, (j + 1) * own)
        out_ref[to, heads * width :, :] = stats[:, here]
        for h in range(heads):
            rows = slice(h * width, (h + 1) * width)
            keep, add = scales[h]
            mixed = acc_ref[h, :, start + j * own : start + (j + 1) * own] * keep[:, here]
            if add is not None:
                mixed = mixed + more_ref[j, rows, :].astype(jnp.float32) * add[:, here]
            out_ref[to, rows, :] = mixed.astype(jnp.bfloat16)


def pack(dest, state, heads, own, start=0, more=None):
    acc, stat = state
    width, count = acc.shape[1], acc.shape[2]
    more = () if more is None else (more,)
    return pl.pallas_call(
        functools.partial(pack_kernel, heads=heads, width=width, own=own, start=start),
        out_shape=jax.ShapeDtypeStruct(
            ((count - start) // own, heads * width + STAT_ROWS, own), jnp.bfloat16
        ),
        in_specs=[SMEM, VMEM, VMEM] + [VMEM] * len(more),
        out_specs=VMEM,
        compiler_params=pltpu.CompilerParams(vmem_limit_bytes=4 * 2**20),
        name="pack",
    )(dest, acc, stat, *more)


def merge_kernel(in_ref, out_ref, *, heads, width):
    sources = in_ref.shape[0]
    for h in range(heads):
        logs = [
            log_weight(in_ref[i, heads * width :, :].astype(jnp.float32), h) for i in range(sources)
        ]
        top = functools.reduce(jnp.maximum, logs)
        shares = [jnp.exp2(x - top) for x in logs]
        total = functools.reduce(jnp.add, shares)
        mixed = None
        for i in range(sources):
            part = in_ref[i, h * width : (h + 1) * width, :].astype(jnp.float32) * (shares[i] / total)
            mixed = part if mixed is None else mixed + part
        out_ref[:, h * width : (h + 1) * width] = mixed.T.astype(jnp.bfloat16)


def merge(parts, heads, width):
    return pl.pallas_call(
        functools.partial(merge_kernel, heads=heads, width=width),
        out_shape=jax.ShapeDtypeStruct((parts.shape[2], heads * width), jnp.bfloat16),
        in_specs=[VMEM],
        out_specs=VMEM,
        compiler_params=pltpu.CompilerParams(vmem_limit_bytes=4 * 2**20),
        name="merge",
    )(parts)


def body(queries, keys, values):
    own, heads, width = queries.shape
    n_x, n_z, n_col = (lax.axis_size(a) for a in ("x", "z", "col"))
    swap = functools.partial(lax.ppermute, axis_name="col", perm=[(c, n_col - 1 - c) for c in range(n_col)])
    along = [
        (z * n_col + c, (z + (1 if c == 0 else -1)) % n_z * n_col + c)
        for z in range(n_z)
        for c in range(n_col)
    ]
    forward = functools.partial(lax.ppermute, axis_name=("z", "col"), perm=along)
    here = jnp.concatenate([keys, values], axis=0).reshape(2 * own, heads * width)
    q = lax.optimization_barrier((queries, here))[0].reshape(own, heads * width)
    ahead = forward(here)
    other = swap(here)
    chunk = [ahead, forward(other)]

    q_mine = [q]
    for d in (1, n_x - 1, *range(2, n_x - 1)):
        q_mine.append(lax.ppermute(q, "x", [(x, (x + d) % n_x) for x in range(n_x)]))
    offsets = [0, 1, n_x - 1, *range(2, n_x - 1)]
    q_theirs = [swap(a) for a in q_mine]
    q_all = lay(q_mine + q_theirs, heads)

    state = fold(None, [here, *chunk], q_all)
    last = n_z // 2
    for _ in range(2, last):
        chunk = [forward(a) for a in chunk]
        state = fold(state, chunk, q_all)
    share = q_all.shape[1] // n_col
    sent = swap(pack(jnp.arange(n_x, dtype=jnp.int32), state, heads, own, start=share))
    chunk = forward(chunk[0])
    other = swap(chunk)
    mine = fold(state, [chunk, other], q_all, share)

    x = lax.axis_index("x")
    dest = jnp.stack([x - d for d in offsets]) % n_x
    parts = pack(dest.astype(jnp.int32), mine, heads, own, more=sent)
    parts = lax.all_to_all(parts, "x", 0, 0, tiled=True)
    return merge(parts, heads, width)


def solution(mesh):
    n_grp, n_row, n_col = mesh.devices.shape
    n_z = n_row // ROW_X
    split = Mesh(mesh.devices.reshape(n_grp, ROW_X, n_z, n_col), ("grp", "x", "z", "col"))
    everywhere = ("grp", "x", "z", "col")

    return jax.shard_map(
        body,
        mesh=split,
        in_specs=(P(everywhere, None, None),) * 3,
        out_specs=P(everywhere, None),
        check_vma=False,
    )
```

time: 361 us -> 114 us (0.32)
  waiting for transfers between devices: 178 us -> 5.64 us
  matrix products: 72.4 us -> 0 us
  other arithmetic: 41 us -> 1.39 us
  starting transfers between devices: 23.9 us -> 63.2 us
  Pallas kernels: 0 us -> 30.5 us
  local copies, waits for them, and re-layouts: 23.3 us -> 0.96 us
  between operations: 13.5 us -> 0.16 us
  blocking collectives: 7.53 us -> 11.8 us
    all_gather x1 -> x0, waiting for transfers between devices: 177 us -> none  [side_by_side(): result = lax.all_gather(both, axis, axis=dim, tiled=True)]
    dot_general x16 -> x0, matrix products: 72.4 us -> none  [the longest x8 45.6 us: advance(): jnp.einsum('qhd,khd->hqk', query_rows, key_block, preferred_element_type=...]
    ppermute x0 -> x25, starting transfers between devices: none -> 63.2 us  [the longest x12 26.7 us: body(): chunk = [forward(a) for a in chunk]]
    reduce_sum x9 -> x0, other arithmetic: 39.6 us -> none  [the longest x8 39.3 us: advance(): summed = summed * factor + jnp.sum(weights.astype(jnp.float32), axis=-1)]
    pallas_call x0 -> x12, Pallas kernels: none -> 30.5 us  [the longest x8 26.6 us: fold(): pl.pallas_call(functools.partial(fold_kernel, pieces=pieces, heads=heads,...]
    all_to_all x1 -> x0, starting transfers between devices: 23.9 us -> none  [copy_for_each(): lax.all_to_all(jnp.broadcast_to(value[None], (devices, *value.shape)), ax...]
    split x1 -> x0, local copies, waits for them, and re-layouts: 11.3 us -> none  [side_by_side(): jnp.split(result, [sum(widths[:k]) for k in range(1, len(widths))], axis=...]
    all_to_all x1, blocking collectives: 3.94 us -> 11.8 us  [body(): parts = lax.all_to_all(parts, 'x', 0, 0, tiled=True)]
  transfers between devices with their start and end apart: 2 -> 25, of which waited for: 2 -> 5; matrix products, arithmetic and copies ran while one was open for 0% -> 1% of each run, Pallas kernels for 0% -> 25%
where the time goes in v1:
time: 114 us
  starting transfers between devices  63.2 us (55%)
  Pallas kernels  30.5 us (27%)
  blocking collectives  11.8 us (10%)
  waiting for transfers between devices  5.64 us (5%)
  other arithmetic  1.39 us (1%)
    ppermute x12, starting transfers between devices, body(): chunk = [forward(a) for a in chunk]  26.7 us
    pallas_call x8, Pallas kernels, fold(): pl.pallas_call(functools.partial(fold_kernel, pieces=pieces, heads=heads,...  26.6 us
    ppermute x1, starting transfers between devices, body(): other = swap(here)  20.5 us
    all_to_all x1, blocking collectives, body(): parts = lax.all_to_all(parts, 'x', 0, 0, tiled=True)  11.8 us
    ppermute x4, starting transfers between devices, body(): q_theirs = [swap(a) for a in q_mine]  5 us
    ppermute x3, starting transfers between devices, body(): lax.ppermute(q, 'x', [(x, (x + d) % n_x) for x in range(n_x)])  4.59 us
    ppermute x1, starting transfers between devices, body(): ahead = forward(here)  3.11 us
    pallas_call x2, Pallas kernels, pack(): pl.pallas_call(functools.partial(pack_kernel, heads=heads, width=width, o...  2.86 us
  transfers between devices with their start and end apart: 25, of which 5 were waited for; matrix products, arithmetic and copies ran while one was open for 1% of the time, Pallas kernels for 25%

profile of v1, /device:TPU:33, one launch (start us, length us, event | category | flops | bytes accessed | tf_op | source)
XLA Modules:
  0.0 113.7 jit_solution(10264958839048010372)
XLA Ops:
  1.4 20.5 %collective-permute-start.16 = (bf16[512,256]{1,0:T(8,128)(2,1)S(1)}, bf16[512,256]{1,0:T(8,128)(2,1)S(1)}, u32[]{:S(2)}, u32[]{:S(2)}) collective-permute-start(bf16[512,256]{1,0:T(8,128)(2,1)S(1)} %bitcast.17), channel_id=1, source_target_pairs={{0,1},{1,0},{2,3},{3,2},{4,5},{5,4},{6,7},{7,6},{8,9},{9,8},{10,11... | collective-permute-start | bytes 786440 | tf_op jit(solution)/shard_map/ppermute | solution.py:228
  21.9 3.1 %collective-permute-start = (bf16[512,256]{1,0:T(8,128)(2,1)S(1)}, bf16[512,256]{1,0:T(8,128)(2,1)S(1)}, u32[]{:S(2)}, u32[]{:S(2)}) collective-permute-start(bf16[512,256]{1,0:T(8,128)(2,1)S(1)} %bitcast.18), channel_id=1, source_target_pairs={{0,2},{1,31},{2,4},{3,1},{4,6},{5,3},{6,8},{7,5},{8,10},{9,7},{10,... | collective-permute-start | bytes 786440 | tf_op jit(solution)/shard_map/ppermute | solution.py:227
  26.2 2.2 %collective-permute-done.refs_1_ = bf16[512,256]{1,0:T(8,128)(2,1)S(1)} collective-permute-done((bf16[512,256]{1,0:T(8,128)(2,1)S(1)}, bf16[512,256]{1,0:T(8,128)(2,1)S(1)}, u32[]{:S(2)}, u32[]{:S(2)}) %collective-permute-start) | collective-permute-done | bytes 262176 | tf_op jit(solution)/shard_map/ppermute | solution.py:227
  28.3 3.1 %collective-permute-start.1 = (bf16[512,256]{1,0:T(8,128)(2,1)S(1)}, bf16[512,256]{1,0:T(8,128)(2,1)S(1)}, u32[]{:S(2)}, u32[]{:S(2)}) collective-permute-start(bf16[512,256]{1,0:T(8,128)(2,1)S(1)} %collective-permute-done.refs_1_), channel_id=1, source_target_pairs={{0,2},{1,31},{2,4},{3,1},{4,6},{5,3},{6,8},{7,5},{8,10},{9,7},{10,... | collective-permute-start | bytes 786440 | tf_op jit(solution)/shard_map/ppermute | solution.py:241
  31.4 2.8 %collective-permute-start.18 = (bf16[512,256]{1,0:T(8,128)(2,1)S(1)}, bf16[512,256]{1,0:T(8,128)(2,1)S(1)}, u32[]{:S(2)}, u32[]{:S(2)}) collective-permute-start(bf16[512,256]{1,0:T(8,128)(2,1)S(1)} %collective-permute-done.17.refs_2_), channel_id=1, source_target_pairs={{0,2},{1,31},{2,4},{3,1},{4,6},{5,3},{6,8},{7,5},{8,10},{9,7},{10,... | collective-permute-start | bytes 786440 | tf_op jit(solution)/shard_map/ppermute | solution.py:241
  34.8 3.1 %collective-permute-start.2 = (bf16[512,256]{1,0:T(8,128)(2,1)S(1)}, bf16[512,256]{1,0:T(8,128)(2,1)S(1)}, u32[]{:S(2)}, u32[]{:S(2)}) collective-permute-start(bf16[512,256]{1,0:T(8,128)(2,1)S(1)} %collective-permute-done.1.refs_0_), channel_id=1, source_target_pairs={{0,2},{1,31},{2,4},{3,1},{4,6},{5,3},{6,8},{7,5},{8,10},{9,7},{10,... | collective-permute-start | bytes 786440 | tf_op jit(solution)/shard_map/ppermute | solution.py:241
  37.9 2.8 %collective-permute-start.19 = (bf16[512,256]{1,0:T(8,128)(2,1)S(1)}, bf16[512,256]{1,0:T(8,128)(2,1)S(1)}, u32[]{:S(2)}, u32[]{:S(2)}) collective-permute-start(bf16[512,256]{1,0:T(8,128)(2,1)S(1)} %collective-permute-done.18.refs_1_), channel_id=1, source_target_pairs={{0,2},{1,31},{2,4},{3,1},{4,6},{5,3},{6,8},{7,5},{8,10},{9,7},{10,... | collective-permute-start | bytes 786440 | tf_op jit(solution)/shard_map/ppermute | solution.py:241
  41.2 3.1 %collective-permute-start.3 = (bf16[512,256]{1,0:T(8,128)(2,1)S(1)}, bf16[512,256]{1,0:T(8,128)(2,1)S(1)}, u32[]{:S(2)}, u32[]{:S(2)}) collective-permute-start(bf16[512,256]{1,0:T(8,128)(2,1)S(1)} %collective-permute-done.2.refs_0_), channel_id=1, source_target_pairs={{0,2},{1,31},{2,4},{3,1},{4,6},{5,3},{6,8},{7,5},{8,10},{9,7},{10,... | collective-permute-start | bytes 786440 | tf_op jit(solution)/shard_map/ppermute | solution.py:241
  44.3 2.8 %collective-permute-start.20 = (bf16[512,256]{1,0:T(8,128)(2,1)S(1)}, bf16[512,256]{1,0:T(8,128)(2,1)S(1)}, u32[]{:S(2)}, u32[]{:S(2)}) collective-permute-start(bf16[512,256]{1,0:T(8,128)(2,1)S(1)} %collective-permute-done.19.refs_1_), channel_id=1, source_target_pairs={{0,2},{1,31},{2,4},{3,1},{4,6},{5,3},{6,8},{7,5},{8,10},{9,7},{10,... | collective-permute-start | bytes 786440 | tf_op jit(solution)/shard_map/ppermute | solution.py:241
  50.7 2.9 %collective-permute-start.10 = (bf16[256,256]{1,0:T(8,128)(2,1)S(1)}, bf16[256,256]{1,0:T(8,128)(2,1)S(1)}, u32[]{:S(2)}, u32[]{:S(2)}) collective-permute-start(bf16[256,256]{1,0:T(8,128)(2,1)S(1)} %bitcast.13), channel_id=1, source_target_pairs={{0,96},{32,0},{64,32},{96,64},{1,97},{33,1},{65,33},{97,65},{2,98}... | collective-permute-start | bytes 393224 | tf_op jit(solution)/shard_map/ppermute | solution.py:233
  54.2 2.0 %collective-permute-start.12 = (bf16[256,256]{1,0:T(8,128)(2,1)S(1)}, bf16[256,256]{1,0:T(8,128)(2,1)S(1)}, u32[]{:S(2)}, u32[]{:S(2)}) collective-permute-start(bf16[256,256]{1,0:T(8,128)(2,1)S(1)} %bitcast.15), channel_id=1, source_target_pairs={{0,1},{1,0},{2,3},{3,2},{4,5},{5,4},{6,7},{7,6},{8,9},{9,8},{10,11... | collective-permute-start | bytes 393224 | tf_op jit(solution)/shard_map/ppermute | solution.py:235
  56.2 3.0 %collective-permute-start.21 = (bf16[512,256]{1,0:T(8,128)(2,1)S(1)}, bf16[512,256]{1,0:T(8,128)(2,1)S(1)}, u32[]{:S(2)}, u32[]{:S(2)}) collective-permute-start(bf16[512,256]{1,0:T(8,128)(2,1)S(1)} %collective-permute-done.20.refs_1_), channel_id=1, source_target_pairs={{0,2},{1,31},{2,4},{3,1},{4,6},{5,3},{6,8},{7,5},{8,10},{9,7},{10,... | collective-permute-start | bytes 786440 | tf_op jit(solution)/shard_map/ppermute | solution.py:241
  60.3 1.9 %collective-permute-start.14 = (bf16[256,256]{1,0:T(8,128)(2,1)S(1)}, bf16[256,256]{1,0:T(8,128)(2,1)S(1)}, u32[]{:S(2)}, u32[]{:S(2)}) collective-permute-start(bf16[256,256]{1,0:T(8,128)(2,1)S(1)} %collective-permute-done.10.refs_2_), channel_id=1, source_target_pairs={{0,1},{1,0},{2,3},{3,2},{4,5},{5,4},{6,7},{7,6},{8,9},{9,8},{10,11... | collective-permute-start | bytes 393224 | tf_op jit(solution)/shard_map/ppermute | solution.py:235
  62.2 3.1 %collective-permute-start.5 = (bf16[512,256]{1,0:T(8,128)(2,1)S(1)}, bf16[512,256]{1,0:T(8,128)(2,1)S(1)}, u32[]{:S(2)}, u32[]{:S(2)}) collective-permute-start(bf16[512,256]{1,0:T(8,128)(2,1)S(1)} %collective-permute-done.4.refs_0_), channel_id=1, source_target_pairs={{0,2},{1,31},{2,4},{3,1},{4,6},{5,3},{6,8},{7,5},{8,10},{9,7},{10,... | collective-permute-start | bytes 786440 | tf_op jit(solution)/shard_map/ppermute | solution.py:241
  66.8 4.4 %fold.8 = (f32[2,128,2048]{2,1,0:T(8,128)S(1)}, f32[2,8,2048]{2,1,0:T(8,128)S(1)}) custom-call(bf16[512,256]{1,0:T(8,128)(2,1)S(1)} %bitcast.19, bf16[512,256]{1,0:T(8,128)(2,1)S(1)} %collective-permute-done.refs_1_, bf16[512,256]{1,0:T(8,128)(2,1)S(1)} %collective-permute-done.17.refs_2_, bf16[2,2048,128]{2,1,0:T(8,128)(2,1)S(1)} %lay.1.refs_3_.refs_2_), custom_call_target="tpu_custom_call" | custom-call | flops 1610612736 | tf_op jit(solution)/shard_map/fold/pallas_call | solution.py:84
  71.2 3.3 %fold.9 = (f32[2,128,2048]{2,1,0:T(8,128)S(1)}, f32[2,8,2048]{2,1,0:T(8,128)S(1)}) custom-call(bf16[512,256]{1,0:T(8,128)(2,1)S(1)} %collective-permute-done.1.refs_0_, bf16[512,256]{1,0:T(8,128)(2,1)S(1)} %collective-permute-done.18.refs_1_, bf16[2,2048,128]{2,1,0:T(8,128)(2,1)S(1)} %lay.1.refs_3_.refs_2_, ...), custom_call_target="tpu_custom_call", output_to_operand_aliasing={{0}: (3, {}), {1}: (4, {})} | custom-call | flops 1073741824 | tf_op jit(solution)/shard_map/fold/pallas_call | solution.py:84
  74.7 3.2 %fold.10 = (f32[2,128,2048]{2,1,0:T(8,128)S(1)}, f32[2,8,2048]{2,1,0:T(8,128)S(1)}) custom-call(bf16[512,256]{1,0:T(8,128)(2,1)S(1)} %collective-permute-done.2.refs_0_, bf16[512,256]{1,0:T(8,128)(2,1)S(1)} %collective-permute-done.19.refs_1_, bf16[2,2048,128]{2,1,0:T(8,128)(2,1)S(1)} %lay.1.refs_3_.refs_2_, ...), custom_call_target="tpu_custom_call", output_to_operand_aliasing={{0}: (3, {}), {1}: (4, {})} | custom-call | flops 1073741824 | tf_op jit(solution)/shard_map/fold/pallas_call | solution.py:84
  78.1 3.2 %fold.11 = (f32[2,128,2048]{2,1,0:T(8,128)S(1)}, f32[2,8,2048]{2,1,0:T(8,128)S(1)}) custom-call(bf16[512,256]{1,0:T(8,128)(2,1)S(1)} %collective-permute-done.3.refs_0_, bf16[512,256]{1,0:T(8,128)(2,1)S(1)} %collective-permute-done.20.refs_1_, bf16[2,2048,128]{2,1,0:T(8,128)(2,1)S(1)} %lay.1.refs_3_.refs_2_, ...), custom_call_target="tpu_custom_call", output_to_operand_aliasing={{0}: (3, {}), {1}: (4, {})} | custom-call | flops 1073741824 | tf_op jit(solution)/shard_map/fold/pallas_call | solution.py:84
  81.3 3.2 %fold.12 = (f32[2,128,2048]{2,1,0:T(8,128)S(1)}, f32[2,8,2048]{2,1,0:T(8,128)S(1)}) custom-call(bf16[512,256]{1,0:T(8,128)(2,1)S(1)} %collective-permute-done.4.refs_0_, bf16[512,256]{1,0:T(8,128)(2,1)S(1)} %collective-permute-done.21.refs_1_, bf16[2,2048,128]{2,1,0:T(8,128)(2,1)S(1)} %lay.1.refs_3_.refs_2_, ...), custom_call_target="tpu_custom_call", output_to_operand_aliasing={{0}: (3, {}), {1}: (4, {})} | custom-call | flops 1073741824 | tf_op jit(solution)/shard_map/fold/pallas_call | solution.py:84
  86.2 3.2 %fold.13 = (f32[2,128,2048]{2,1,0:T(8,128)S(1)}, f32[2,8,2048]{2,1,0:T(8,128)S(1)}) custom-call(bf16[512,256]{1,0:T(8,128)(2,1)S(1)} %collective-permute-done.5.refs_0_, bf16[512,256]{1,0:T(8,128)(2,1)S(1)} %collective-permute-done.22.refs_1_, bf16[2,2048,128]{2,1,0:T(8,128)(2,1)S(1)} %lay.1.refs_3_.refs_2_, ...), custom_call_target="tpu_custom_call", output_to_operand_aliasing={{0}: (3, {}), {1}: (4, {})} | custom-call | flops 1073741824 | tf_op jit(solution)/shard_map/fold/pallas_call | solution.py:84
  89.4 3.3 %fold.14 = (f32[2,128,2048]{2,1,0:T(8,128)S(1)}, f32[2,8,2048]{2,1,0:T(8,128)S(1)}) custom-call(bf16[512,256]{1,0:T(8,128)(2,1)S(1)} %collective-permute-done.6.refs_0_, bf16[512,256]{1,0:T(8,128)(2,1)S(1)} %collective-permute-done.23.refs_1_, bf16[2,2048,128]{2,1,0:T(8,128)(2,1)S(1)} %lay.1.refs_3_.refs_2_, ...), custom_call_target="tpu_custom_call", output_to_operand_aliasing={{0}: (3, {}), {1}: (4, {})} | custom-call | flops 1073741824 | tf_op jit(solution)/shard_map/fold/pallas_call | solution.py:84
  94.8 2.1 %collective-permute-done.8.refs_1_ = bf16[512,256]{1,0:T(8,128)(2,1)} collective-permute-done((bf16[512,256]{1,0:T(8,128)(2,1)S(1)}, bf16[512,256]{1,0:T(8,128)(2,1)}, u32[]{:S(2)}, u32[]{:S(2)}) %collective-permute-start.8) | collective-permute-done | bytes 262176 | tf_op jit(solution)/shard_map/ppermute | solution.py:246
  96.9 2.7 %fold.15 = (f32[2,128,1024]{2,1,0:T(8,128)S(1)}, f32[2,8,1024]{2,1,0:T(8,128)S(1)}) custom-call(bf16[512,256]{1,0:T(8,128)(2,1)S(1)} %collective-permute-done.7.refs_0_, bf16[512,256]{1,0:T(8,128)(2,1)} %collective-permute-done.8.refs_1_, bf16[2,2048,128]{2,1,0:T(8,128)(2,1)S(1)} %lay.1.refs_3_.refs_2_, ...), custom_call_target="tpu_custom_call" | custom-call | flops 536870912 | tf_op jit(solution)/shard_map/fold/pallas_call | solution.py:84
  101.0 11.8 %all_to_all.5.in_ref = bf16[4,272,256]{2,1,0:T(8,128)(2,1)S(1)} all-to-all(bf16[4,272,256]{2,1,0:T(8,128)(2,1)S(1)} %pack.3), channel_id=1, replica_groups=mesh['grp'=2,'x'=4,'z'=16,'col'=2] {'x'}, dimensions={0} | all-to-all | bytes 1114112 | tf_op jit(solution)/shard_map/all_to_all | solution.py:252
  (44 shorter events, 16.6 us)
Async XLA Ops:
  1.4 23.6 %collective-permute-start.16 = (bf16[512,256]{1,0:T(8,128)(2,1)S(1)}, bf16[512,256]{1,0:T(8,128)(2,1)S(1)}, u32[]{:S(2)}, u32[]{:S(2)}) collective-permute-start(bf16[512,256]{1,0:T(8,128)(2,1)S(1)} %bitcast.17), channel_id=1, source_target_pairs={{0,1},{1,0},{2,3},{3,2},{4,5},{5,4},{6,7},{7,6},{8,9},{9,8},{10,11... | collective-permute-start | bytes 786440 | tf_op jit(solution)/shard_map/ppermute | solution.py:228
  21.9 6.4 %collective-permute-start = (bf16[512,256]{1,0:T(8,128)(2,1)S(1)}, bf16[512,256]{1,0:T(8,128)(2,1)S(1)}, u32[]{:S(2)}, u32[]{:S(2)}) collective-permute-start(bf16[512,256]{1,0:T(8,128)(2,1)S(1)} %bitcast.18), channel_id=1, source_target_pairs={{0,2},{1,31},{2,4},{3,1},{4,6},{5,3},{6,8},{7,5},{8,10},{9,7},{10,... | collective-permute-start | bytes 786440 | tf_op jit(solution)/shard_map/ppermute | solution.py:227
  25.0 6.4 %collective-permute-start.17 = (bf16[512,256]{1,0:T(8,128)(2,1)S(1)}, bf16[512,256]{1,0:T(8,128)(2,1)S(1)}, u32[]{:S(2)}, u32[]{:S(2)}) collective-permute-start(bf16[512,256]{1,0:T(8,128)(2,1)S(1)} %collective-permute-done.16), channel_id=1, source_target_pairs={{0,2},{1,31},{2,4},{3,1},{4,6},{5,3},{6,8},{7,5},{8,10},{9,7},{10,... | collective-permute-start | bytes 786440 | tf_op jit(solution)/shard_map/ppermute | solution.py:229
  28.3 6.4 %collective-permute-start.1 = (bf16[512,256]{1,0:T(8,128)(2,1)S(1)}, bf16[512,256]{1,0:T(8,128)(2,1)S(1)}, u32[]{:S(2)}, u32[]{:S(2)}) collective-permute-start(bf16[512,256]{1,0:T(8,128)(2,1)S(1)} %collective-permute-done.refs_1_), channel_id=1, source_target_pairs={{0,2},{1,31},{2,4},{3,1},{4,6},{5,3},{6,8},{7,5},{8,10},{9,7},{10,... | collective-permute-start | bytes 786440 | tf_op jit(solution)/shard_map/ppermute | solution.py:241
  31.4 6.4 %collective-permute-start.18 = (bf16[512,256]{1,0:T(8,128)(2,1)S(1)}, bf16[512,256]{1,0:T(8,128)(2,1)S(1)}, u32[]{:S(2)}, u32[]{:S(2)}) collective-permute-start(bf16[512,256]{1,0:T(8,128)(2,1)S(1)} %collective-permute-done.17.refs_2_), channel_id=1, source_target_pairs={{0,2},{1,31},{2,4},{3,1},{4,6},{5,3},{6,8},{7,5},{8,10},{9,7},{10,... | collective-permute-start | bytes 786440 | tf_op jit(solution)/shard_map/ppermute | solution.py:241
  34.8 6.4 %collective-permute-start.2 = (bf16[512,256]{1,0:T(8,128)(2,1)S(1)}, bf16[512,256]{1,0:T(8,128)(2,1)S(1)}, u32[]{:S(2)}, u32[]{:S(2)}) collective-permute-start(bf16[512,256]{1,0:T(8,128)(2,1)S(1)} %collective-permute-done.1.refs_0_), channel_id=1, source_target_pairs={{0,2},{1,31},{2,4},{3,1},{4,6},{5,3},{6,8},{7,5},{8,10},{9,7},{10,... | collective-permute-start | bytes 786440 | tf_op jit(solution)/shard_map/ppermute | solution.py:241
  37.9 6.4 %collective-permute-start.19 = (bf16[512,256]{1,0:T(8,128)(2,1)S(1)}, bf16[512,256]{1,0:T(8,128)(2,1)S(1)}, u32[]{:S(2)}, u32[]{:S(2)}) collective-permute-start(bf16[512,256]{1,0:T(8,128)(2,1)S(1)} %collective-permute-done.18.refs_1_), channel_id=1, source_target_pairs={{0,2},{1,31},{2,4},{3,1},{4,6},{5,3},{6,8},{7,5},{8,10},{9,7},{10,... | collective-permute-start | bytes 786440 | tf_op jit(solution)/shard_map/ppermute | solution.py:241
  41.2 8.3 %collective-permute-start.3 = (bf16[512,256]{1,0:T(8,128)(2,1)S(1)}, bf16[512,256]{1,0:T(8,128)(2,1)S(1)}, u32[]{:S(2)}, u32[]{:S(2)}) collective-permute-start(bf16[512,256]{1,0:T(8,128)(2,1)S(1)} %collective-permute-done.2.refs_0_), channel_id=1, source_target_pairs={{0,2},{1,31},{2,4},{3,1},{4,6},{5,3},{6,8},{7,5},{8,10},{9,7},{10,... | collective-permute-start | bytes 786440 | tf_op jit(solution)/shard_map/ppermute | solution.py:241
  44.3 11.9 %collective-permute-start.20 = (bf16[512,256]{1,0:T(8,128)(2,1)S(1)}, bf16[512,256]{1,0:T(8,128)(2,1)S(1)}, u32[]{:S(2)}, u32[]{:S(2)}) collective-permute-start(bf16[512,256]{1,0:T(8,128)(2,1)S(1)} %collective-permute-done.19.refs_1_), channel_id=1, source_target_pairs={{0,2},{1,31},{2,4},{3,1},{4,6},{5,3},{6,8},{7,5},{8,10},{9,7},{10,... | collective-permute-start | bytes 786440 | tf_op jit(solution)/shard_map/ppermute | solution.py:241
  48.0 6.2 %collective-permute-start.9 = (bf16[256,256]{1,0:T(8,128)(2,1)S(1)}, bf16[256,256]{1,0:T(8,128)(2,1)S(1)}, u32[]{:S(2)}, u32[]{:S(2)}) collective-permute-start(bf16[256,256]{1,0:T(8,128)(2,1)S(1)} %bitcast.12), channel_id=1, source_target_pairs={{0,32},{32,64},{64,96},{96,0},{1,33},{33,65},{65,97},{97,1},{2,34}... | collective-permute-start | bytes 393224 | tf_op jit(solution)/shard_map/ppermute | solution.py:233
  49.5 12.7 %collective-permute-start.4 = (bf16[512,256]{1,0:T(8,128)(2,1)S(1)}, bf16[512,256]{1,0:T(8,128)(2,1)S(1)}, u32[]{:S(2)}, u32[]{:S(2)}) collective-permute-start(bf16[512,256]{1,0:T(8,128)(2,1)S(1)} %collective-permute-done.3.refs_0_), channel_id=1, source_target_pairs={{0,2},{1,31},{2,4},{3,1},{4,6},{5,3},{6,8},{7,5},{8,10},{9,7},{10,... | collective-permute-start | bytes 786440 | tf_op jit(solution)/shard_map/ppermute | solution.py:241
  50.7 8.5 %collective-permute-start.10 = (bf16[256,256]{1,0:T(8,128)(2,1)S(1)}, bf16[256,256]{1,0:T(8,128)(2,1)S(1)}, u32[]{:S(2)}, u32[]{:S(2)}) collective-permute-start(bf16[256,256]{1,0:T(8,128)(2,1)S(1)} %bitcast.13), channel_id=1, source_target_pairs={{0,96},{32,0},{64,32},{96,64},{1,97},{33,1},{65,33},{97,65},{2,98}... | collective-permute-start | bytes 393224 | tf_op jit(solution)/shard_map/ppermute | solution.py:233
  53.6 6.6 %collective-permute-start.11 = (bf16[256,256]{1,0:T(8,128)(2,1)S(1)}, bf16[256,256]{1,0:T(8,128)(2,1)S(1)}, u32[]{:S(2)}, u32[]{:S(2)}) collective-permute-start(bf16[256,256]{1,0:T(8,128)(2,1)S(1)} %bitcast.14), channel_id=1, source_target_pairs={{0,64},{32,96},{64,0},{96,32},{1,65},{33,97},{65,1},{97,33},{2,66}... | collective-permute-start | bytes 393224 | tf_op jit(solution)/shard_map/ppermute | solution.py:233
  54.2 8.0 %collective-permute-start.12 = (bf16[256,256]{1,0:T(8,128)(2,1)S(1)}, bf16[256,256]{1,0:T(8,128)(2,1)S(1)}, u32[]{:S(2)}, u32[]{:S(2)}) collective-permute-start(bf16[256,256]{1,0:T(8,128)(2,1)S(1)} %bitcast.15), channel_id=1, source_target_pairs={{0,1},{1,0},{2,3},{3,2},{4,5},{5,4},{6,7},{7,6},{8,9},{9,8},{10,11... | collective-permute-start | bytes 393224 | tf_op jit(solution)/shard_map/ppermute | solution.py:235
  56.2 9.2 %collective-permute-start.21 = (bf16[512,256]{1,0:T(8,128)(2,1)S(1)}, bf16[512,256]{1,0:T(8,128)(2,1)S(1)}, u32[]{:S(2)}, u32[]{:S(2)}) collective-permute-start(bf16[512,256]{1,0:T(8,128)(2,1)S(1)} %collective-permute-done.20.refs_1_), channel_id=1, source_target_pairs={{0,2},{1,31},{2,4},{3,1},{4,6},{5,3},{6,8},{7,5},{8,10},{9,7},{10,... | collective-permute-start | bytes 786440 | tf_op jit(solution)/shard_map/ppermute | solution.py:241
  59.2 6.1 %collective-permute-start.13 = (bf16[256,256]{1,0:T(8,128)(2,1)S(1)}, bf16[256,256]{1,0:T(8,128)(2,1)S(1)}, u32[]{:S(2)}, u32[]{:S(2)}) collective-permute-start(bf16[256,256]{1,0:T(8,128)(2,1)S(1)} %collective-permute-done.9.refs_1_), channel_id=1, source_target_pairs={{0,1},{1,0},{2,3},{3,2},{4,5},{5,4},{6,7},{7,6},{8,9},{9,8},{10,11... | collective-permute-start | bytes 393224 | tf_op jit(solution)/shard_map/ppermute | solution.py:235
  60.3 5.0 %collective-permute-start.14 = (bf16[256,256]{1,0:T(8,128)(2,1)S(1)}, bf16[256,256]{1,0:T(8,128)(2,1)S(1)}, u32[]{:S(2)}, u32[]{:S(2)}) collective-permute-start(bf16[256,256]{1,0:T(8,128)(2,1)S(1)} %collective-permute-done.10.refs_2_), channel_id=1, source_target_pairs={{0,1},{1,0},{2,3},{3,2},{4,5},{5,4},{6,7},{7,6},{8,9},{9,8},{10,11... | collective-permute-start | bytes 393224 | tf_op jit(solution)/shard_map/ppermute | solution.py:235
  62.2 3.1 %collective-permute-start.15 = (bf16[256,256]{1,0:T(8,128)(2,1)S(1)}, bf16[256,256]{1,0:T(8,128)(2,1)S(1)}, u32[]{:S(2)}, u32[]{:S(2)}) collective-permute-start(bf16[256,256]{1,0:T(8,128)(2,1)S(1)} %collective-permute-done.11.refs_3_), channel_id=1, source_target_pairs={{0,1},{1,0},{2,3},{3,2},{4,5},{5,4},{6,7},{7,6},{8,9},{9,8},{10,11... | collective-permute-start | bytes 393224 | tf_op jit(solution)/shard_map/ppermute | solution.py:235
  62.2 12.3 %collective-permute-start.5 = (bf16[512,256]{1,0:T(8,128)(2,1)S(1)}, bf16[512,256]{1,0:T(8,128)(2,1)S(1)}, u32[]{:S(2)}, u32[]{:S(2)}) collective-permute-start(bf16[512,256]{1,0:T(8,128)(2,1)S(1)} %collective-permute-done.4.refs_0_), channel_id=1, source_target_pairs={{0,2},{1,31},{2,4},{3,1},{4,6},{5,3},{6,8},{7,5},{8,10},{9,7},{10,... | collective-permute-start | bytes 786440 | tf_op jit(solution)/shard_map/ppermute | solution.py:241
  65.5 12.4 %collective-permute-start.22 = (bf16[512,256]{1,0:T(8,128)(2,1)S(1)}, bf16[512,256]{1,0:T(8,128)(2,1)S(1)}, u32[]{:S(2)}, u32[]{:S(2)}) collective-permute-start(bf16[512,256]{1,0:T(8,128)(2,1)S(1)} %collective-permute-done.21.refs_1_), channel_id=1, source_target_pairs={{0,2},{1,31},{2,4},{3,1},{4,6},{5,3},{6,8},{7,5},{8,10},{9,7},{10,... | collective-permute-start | bytes 786440 | tf_op jit(solution)/shard_map/ppermute | solution.py:241
  74.5 10.1 %collective-permute-start.6 = (bf16[512,256]{1,0:T(8,128)(2,1)S(1)}, bf16[512,256]{1,0:T(8,128)(2,1)S(1)}, u32[]{:S(2)}, u32[]{:S(2)}) collective-permute-start(bf16[512,256]{1,0:T(8,128)(2,1)S(1)} %collective-permute-done.5.refs_0_), channel_id=1, source_target_pairs={{0,2},{1,31},{2,4},{3,1},{4,6},{5,3},{6,8},{7,5},{8,10},{9,7},{10,... | collective-permute-start | bytes 786440 | tf_op jit(solution)/shard_map/ppermute | solution.py:241
  77.9 11.5 %collective-permute-start.23 = (bf16[512,256]{1,0:T(8,128)(2,1)S(1)}, bf16[512,256]{1,0:T(8,128)(2,1)S(1)}, u32[]{:S(2)}, u32[]{:S(2)}) collective-permute-start(bf16[512,256]{1,0:T(8,128)(2,1)S(1)} %collective-permute-done.22.refs_1_), channel_id=1, source_target_pairs={{0,2},{1,31},{2,4},{3,1},{4,6},{5,3},{6,8},{7,5},{8,10},{9,7},{10,... | collective-permute-start | bytes 786440 | tf_op jit(solution)/shard_map/ppermute | solution.py:241
  84.6 9.6 %collective-permute-start.7 = (bf16[512,256]{1,0:T(8,128)(2,1)S(1)}, bf16[512,256]{1,0:T(8,128)(2,1)S(1)}, u32[]{:S(2)}, u32[]{:S(2)}) collective-permute-start(bf16[512,256]{1,0:T(8,128)(2,1)S(1)} %collective-permute-done.6.refs_0_), channel_id=1, source_target_pairs={{0,2},{1,31},{2,4},{3,1},{4,6},{5,3},{6,8},{7,5},{8,10},{9,7},{10,... | collective-permute-start | bytes 786440 | tf_op jit(solution)/shard_map/ppermute | solution.py:245
  94.2 5.4 %collective-permute-start.24 = (bf16[4,272,256]{2,1,0:T(8,128)(2,1)}, bf16[4,272,256]{2,1,0:T(8,128)(2,1)}, u32[]{:S(2)}, u32[]{:S(2)}) collective-permute-start(bf16[4,272,256]{2,1,0:T(8,128)(2,1)} %pack.2), channel_id=1, source_target_pairs={{0,1},{1,0},{2,3},{3,2},{4,5},{5,4},{6,7},{7,6},{8,9},{9,8},{10,11... | collective-permute-start | bytes 1671176 | tf_op jit(solution)/shard_map/ppermute | solution.py:244
  (1 other events, 2.7 us)

commit v2 on v1

--- a/solution.py
+++ b/solution.py
@@ -14,7 +14,6 @@
 BLOCK = 512
 STAT_ROWS = 16
 VMEM = pl.BlockSpec(memory_space=pltpu.VMEM)
-SMEM = pl.BlockSpec(memory_space=pltpu.SMEM)
 NT = (((1,), (1,)), ((), ()))
 
 
@@ -79,7 +78,7 @@
     count = everyone if count is None else count
     first = state is None
     operands = [*chunks, queries, *(() if first else state)]
-    aliases = {} if first or count < everyone else {pieces + 1: 0, pieces + 2: 1}
+    aliases = {} if first or count < state[0].shape[2] else {pieces + 1: 0, pieces + 2: 1}
     flops = 4 * heads * width * count * rows * pieces
     return pl.pallas_call(
         functools.partial(
@@ -130,9 +129,8 @@
     return stats[at : at + 1] + stats[at + 1 : at + 2] + stats[at + 2 : at + 3]
 
 
-def pack_kernel(dest_ref, acc_ref, stat_ref, *refs, heads, width, own, start):
-    (more_ref, out_ref) = refs if len(refs) == 2 else (None, refs[0])
-    owners = out_ref.shape[0]
+def pack_kernel(acc_ref, stat_ref, *refs, heads, width, own, start, owners):
+    more_refs, out_refs = refs[:-owners], refs[-owners:]
     count = owners * own
     at = slice(start, start + count)
     which = lax.broadcasted_iota(jnp.int32, (STAT_ROWS, count), 0)
@@ -141,9 +139,9 @@
     for h in range(heads):
         top, total = stat_ref[h, 0:1, at], stat_ref[h, 1:2, at]
         fade = share = None
-        if more_ref is not None:
+        if more_refs:
             log = jnp.concatenate(
-                [log_weight(more_ref[j, heads * width :, :].astype(jnp.float32), h) for j in range(owners)],
+                [log_weight(more_refs[j][heads * width :, :].astype(jnp.float32), h) for j in range(owners)],
                 axis=1,
             )
             raised = jnp.maximum(top, log)
@@ -158,45 +156,44 @@
             rest = rest - rounded
     stats = stats.astype(jnp.bfloat16)
     for j in range(owners):
-        to, here = dest_ref[j], slice(j * own, (j + 1) * own)
-        out_ref[to, heads * width :, :] = stats[:, here]
+        out_ref, here = out_refs[j], slice(j * own, (j + 1) * own)
+        out_ref[heads * width :, :] = stats[:, here]
         for h in range(heads):
             rows = slice(h * width, (h + 1) * width)
             keep, add = scales[h]
             mixed = acc_ref[h, :, start + j * own : start + (j + 1) * own] * keep[:, here]
             if add is not None:
-                mixed = mixed + more_ref[j, rows, :].astype(jnp.float32) * add[:, here]
-            out_ref[to, rows, :] = mixed.astype(jnp.bfloat16)
-
-
-def pack(dest, state, heads, own, start=0, more=None):
+                mixed = mixed + more_refs[j][rows, :].astype(jnp.float32) * add[:, here]
+            out_ref[rows, :] = mixed.astype(jnp.bfloat16)
+
+
+def pack(state, heads, own, start=0, more=()):
     acc, stat = state
     width, count = acc.shape[1], acc.shape[2]
-    more = () if more is None else (more,)
-    return pl.pallas_call(
-        functools.partial(pack_kernel, heads=heads, width=width, own=own, start=start),
-        out_shape=jax.ShapeDtypeStruct(
-            ((count - start) // own, heads * width + STAT_ROWS, own), jnp.bfloat16
-        ),
-        in_specs=[SMEM, VMEM, VMEM] + [VMEM] * len(more),
-        out_specs=VMEM,
+    owners = (count - start) // own
+    message = jax.ShapeDtypeStruct((heads * width + STAT_ROWS, own), jnp.bfloat16)
+    return pl.pallas_call(
+        functools.partial(pack_kernel, heads=heads, width=width, own=own, start=start, owners=owners),
+        out_shape=(message,) * owners,
+        in_specs=[VMEM] * (2 + len(more)),
+        out_specs=(VMEM,) * owners,
         compiler_params=pltpu.CompilerParams(vmem_limit_bytes=4 * 2**20),
         name="pack",
-    )(dest, acc, stat, *more)
-
-
-def merge_kernel(in_ref, out_ref, *, heads, width):
-    sources = in_ref.shape[0]
+    )(acc, stat, *more)
+
+
+def merge_kernel(*refs, heads, width):
+    in_refs, out_ref = refs[:-1], refs[-1]
     for h in range(heads):
         logs = [
-            log_weight(in_ref[i, heads * width :, :].astype(jnp.float32), h) for i in range(sources)
+            log_weight(part[heads * width :, :].astype(jnp.float32), h) for part in in_refs
         ]
         top = functools.reduce(jnp.maximum, logs)
         shares = [jnp.exp2(x - top) for x in logs]
         total = functools.reduce(jnp.add, shares)
         mixed = None
-        for i in range(sources):
-            part = in_ref[i, h * width : (h + 1) * width, :].astype(jnp.float32) * (shares[i] / total)
+        for ref, share in zip(in_refs, shares):
+            part = ref[h * width : (h + 1) * width, :].astype(jnp.float32) * (share / total)
             mixed = part if mixed is None else mixed + part
         out_ref[:, h * width : (h + 1) * width] = mixed.T.astype(jnp.bfloat16)
 
@@ -204,12 +201,12 @@
 def merge(parts, heads, width):
     return pl.pallas_call(
         functools.partial(merge_kernel, heads=heads, width=width),
-        out_shape=jax.ShapeDtypeStruct((parts.shape[2], heads * width), jnp.bfloat16),
-        in_specs=[VMEM],
+        out_shape=jax.ShapeDtypeStruct((parts[0].shape[1], heads * width), jnp.bfloat16),
+        in_specs=[VMEM] * len(parts),
         out_specs=VMEM,
         compiler_params=pltpu.CompilerParams(vmem_limit_bytes=4 * 2**20),
         name="merge",
-    )(parts)
+    )(*parts)
 
 
 def body(queries, keys, values):
@@ -238,18 +235,21 @@
     state = fold(None, [here, *chunk], q_all)
     last = n_z // 2
     for _ in range(2, last):
-        chunk = [forward(a) for a in chunk]
+        near = forward(chunk[0])
+        chunk = [near, forward(chunk[1])]
         state = fold(state, chunk, q_all)
     share = q_all.shape[1] // n_col
-    sent = swap(pack(jnp.arange(n_x, dtype=jnp.int32), state, heads, own, start=share))
+    sent = [swap(a) for a in pack(state, heads, own, start=share)]
     chunk = forward(chunk[0])
     other = swap(chunk)
-    mine = fold(state, [chunk, other], q_all, share)
-
-    x = lax.axis_index("x")
-    dest = jnp.stack([x - d for d in offsets]) % n_x
-    parts = pack(dest.astype(jnp.int32), mine, heads, own, more=sent)
-    parts = lax.all_to_all(parts, "x", 0, 0, tiled=True)
+    mine = fold(state, [chunk], q_all, share)
+    mine = fold(mine, [other], q_all, share)
+
+    parts = pack(mine, heads, own, more=sent)
+    parts = [parts[0]] + [
+        lax.ppermute(a, "x", [(x, (x - d) % n_x) for x in range(n_x)])
+        for d, a in zip(offsets[1:], parts[1:])
+    ]
     return merge(parts, heads, width)
 
 

time: 114 us -> 114 us (level)
  blocking collectives: 11.8 us -> 0 us
  waiting for transfers between devices: 5.64 us -> 13.8 us
  starting transfers between devices: 63.2 us -> 69.1 us
  Pallas kernels: 30.5 us -> 27.9 us
    ppermute x1, starting transfers between devices: 20.5 us -> 0.01 us  [body(): other = swap(here)]
    ppermute x1, starting transfers between devices: 3.11 us -> 23 us  [body(): ahead = forward(here)]
    all_to_all x1 -> x0, blocking collectives: 11.8 us -> none  [body(): parts = lax.all_to_all(parts, 'x', 0, 0, tiled=True)]
    ppermute x13 -> x19, waiting for transfers between devices: 1.04 us -> 10.4 us  [the longest x3 6.1 us: body(): lax.ppermute(a, 'x', [(x, (x - d) % n_x) for x in range(n_x)])]
    ppermute x13 -> x19, starting transfers between devices: 26.7 us -> 34.1 us  [the longest x6 16.8 us: body(): near = forward(chunk[0])]
    pallas_call x2, Pallas kernels: 2.86 us -> 0.36 us  [pack(): pl.pallas_call(functools.partial(pack_kernel, heads=heads, width=width, o...]
    ppermute x1, waiting for transfers between devices: 2.08 us -> 0.01 us  [body(): other = swap(chunk)]
    ppermute x4, starting transfers between devices: 5 us -> 6.81 us  [body(): q_theirs = [swap(a) for a in q_mine]]
  transfers between devices with their start and end apart: 25 -> 31, of which waited for: 5 -> 7; matrix products, arithmetic and copies ran while one was open for 1% -> 1% of each run, Pallas kernels for 25% -> 24%
where the time goes in v2:
time: 114 us; the launch traced here: 113 us
  starting transfers between devices  69.1 us (61%)
  Pallas kernels  27.9 us (24%)
  waiting for transfers between devices  13.8 us (12%)
  other arithmetic  1.31 us (1%)
    pallas_call x9, Pallas kernels, fold(): pl.pallas_call(functools.partial(fold_kernel, pieces=pieces, heads=heads,...  26.5 us
    ppermute x1, starting transfers between devices, body(): ahead = forward(here)  23 us
    ppermute x6, starting transfers between devices, body(): near = forward(chunk[0])  16.8 us
    ppermute x6, starting transfers between devices, body(): chunk = [near, forward(chunk[1])]  13 us
    ppermute x4, starting transfers between devices, body(): q_theirs = [swap(a) for a in q_mine]  6.81 us
    ppermute x3, waiting for transfers between devices, body(): lax.ppermute(a, 'x', [(x, (x - d) % n_x) for x in range(n_x)])  6.1 us
    ppermute x3, starting transfers between devices, body(): lax.ppermute(q, 'x', [(x, (x + d) % n_x) for x in range(n_x)])  4.59 us
    ppermute x6, waiting for transfers between devices, body(): near = forward(chunk[0])  4.32 us
  transfers between devices with their start and end apart: 31, of which 7 were waited for; matrix products, arithmetic and copies ran while one was open for 1% of the time, Pallas kernels for 24%

profile of v2, /device:TPU:33, one launch (start us, length us, event | category | flops | bytes accessed | tf_op | source)
XLA Modules:
  0.0 113.3 jit_solution(12197904555176267430)
XLA Ops:
  1.4 23.0 %collective-permute-start = (bf16[512,256]{1,0:T(8,128)(2,1)S(1)}, bf16[512,256]{1,0:T(8,128)(2,1)S(1)}, u32[]{:S(2)}, u32[]{:S(2)}) collective-permute-start(bf16[512,256]{1,0:T(8,128)(2,1)S(1)} %bitcast.13), channel_id=1, source_target_pairs={{0,2},{1,31},{2,4},{3,1},{4,6},{5,3},{6,8},{7,5},{8,10},{9,7},{10,... | collective-permute-start | bytes 786440 | tf_op jit(solution)/shard_map/ppermute | solution.py:224
  24.4 3.3 %collective-permute-done.refs_1_ = bf16[512,256]{1,0:T(8,128)(2,1)S(1)} collective-permute-done((bf16[512,256]{1,0:T(8,128)(2,1)S(1)}, bf16[512,256]{1,0:T(8,128)(2,1)S(1)}, u32[]{:S(2)}, u32[]{:S(2)}) %collective-permute-start) | collective-permute-done | bytes 262176 | tf_op jit(solution)/shard_map/ppermute | solution.py:224
  27.7 3.1 %collective-permute-start.1 = (bf16[512,256]{1,0:T(8,128)(2,1)S(1)}, bf16[512,256]{1,0:T(8,128)(2,1)S(1)}, u32[]{:S(2)}, u32[]{:S(2)}) collective-permute-start(bf16[512,256]{1,0:T(8,128)(2,1)S(1)} %collective-permute-done.refs_1_), channel_id=1, source_target_pairs={{0,2},{1,31},{2,4},{3,1},{4,6},{5,3},{6,8},{7,5},{8,10},{9,7},{10,... | collective-permute-start | bytes 786440 | tf_op jit(solution)/shard_map/ppermute | solution.py:238
  30.8 3.3 %collective-permute-done.1.refs_0_ = bf16[512,256]{1,0:T(8,128)(2,1)S(1)} collective-permute-done((bf16[512,256]{1,0:T(8,128)(2,1)S(1)}, bf16[512,256]{1,0:T(8,128)(2,1)S(1)}, u32[]{:S(2)}, u32[]{:S(2)}) %collective-permute-start.1) | collective-permute-done | bytes 262176 | tf_op jit(solution)/shard_map/ppermute | solution.py:238
  34.1 3.1 %collective-permute-start.2 = (bf16[512,256]{1,0:T(8,128)(2,1)S(1)}, bf16[512,256]{1,0:T(8,128)(2,1)S(1)}, u32[]{:S(2)}, u32[]{:S(2)}) collective-permute-start(bf16[512,256]{1,0:T(8,128)(2,1)S(1)} %collective-permute-done.1.refs_0_), channel_id=1, source_target_pairs={{0,2},{1,31},{2,4},{3,1},{4,6},{5,3},{6,8},{7,5},{8,10},{9,7},{10,... | collective-permute-start | bytes 786440 | tf_op jit(solution)/shard_map/ppermute | solution.py:238
  37.3 2.8 %collective-permute-start.18 = (bf16[512,256]{1,0:T(8,128)(2,1)S(1)}, bf16[512,256]{1,0:T(8,128)(2,1)S(1)}, u32[]{:S(2)}, u32[]{:S(2)}) collective-permute-start(bf16[512,256]{1,0:T(8,128)(2,1)S(1)} %collective-permute-done.17.refs_2_), channel_id=1, source_target_pairs={{0,2},{1,31},{2,4},{3,1},{4,6},{5,3},{6,8},{7,5},{8,10},{9,7},{10,... | collective-permute-start | bytes 786440 | tf_op jit(solution)/shard_map/ppermute | solution.py:239
  40.6 3.1 %collective-permute-start.3 = (bf16[512,256]{1,0:T(8,128)(2,1)S(1)}, bf16[512,256]{1,0:T(8,128)(2,1)S(1)}, u32[]{:S(2)}, u32[]{:S(2)}) collective-permute-start(bf16[512,256]{1,0:T(8,128)(2,1)S(1)} %collective-permute-done.2.refs_0_), channel_id=1, source_target_pairs={{0,2},{1,31},{2,4},{3,1},{4,6},{5,3},{6,8},{7,5},{8,10},{9,7},{10,... | collective-permute-start | bytes 786440 | tf_op jit(solution)/shard_map/ppermute | solution.py:238
  43.7 2.8 %collective-permute-start.19 = (bf16[512,256]{1,0:T(8,128)(2,1)S(1)}, bf16[512,256]{1,0:T(8,128)(2,1)S(1)}, u32[]{:S(2)}, u32[]{:S(2)}) collective-permute-start(bf16[512,256]{1,0:T(8,128)(2,1)S(1)} %collective-permute-done.18.refs_1_), channel_id=1, source_target_pairs={{0,2},{1,31},{2,4},{3,1},{4,6},{5,3},{6,8},{7,5},{8,10},{9,7},{10,... | collective-permute-start | bytes 786440 | tf_op jit(solution)/shard_map/ppermute | solution.py:239
  47.0 3.1 %collective-permute-start.4 = (bf16[512,256]{1,0:T(8,128)(2,1)S(1)}, bf16[512,256]{1,0:T(8,128)(2,1)S(1)}, u32[]{:S(2)}, u32[]{:S(2)}) collective-permute-start(bf16[512,256]{1,0:T(8,128)(2,1)S(1)} %collective-permute-done.3.refs_0_), channel_id=1, source_target_pairs={{0,2},{1,31},{2,4},{3,1},{4,6},{5,3},{6,8},{7,5},{8,10},{9,7},{10,... | collective-permute-start | bytes 786440 | tf_op jit(solution)/shard_map/ppermute | solution.py:238
  50.1 2.8 %collective-permute-start.20 = (bf16[512,256]{1,0:T(8,128)(2,1)S(1)}, bf16[512,256]{1,0:T(8,128)(2,1)S(1)}, u32[]{:S(2)}, u32[]{:S(2)}) collective-permute-start(bf16[512,256]{1,0:T(8,128)(2,1)S(1)} %collective-permute-done.19.refs_1_), channel_id=1, source_target_pairs={{0,2},{1,31},{2,4},{3,1},{4,6},{5,3},{6,8},{7,5},{8,10},{9,7},{10,... | collective-permute-start | bytes 786440 | tf_op jit(solution)/shard_map/ppermute | solution.py:239
  56.6 2.9 %collective-permute-start.10 = (bf16[256,256]{1,0:T(8,128)(2,1)S(1)}, bf16[256,256]{1,0:T(8,128)(2,1)S(1)}, u32[]{:S(2)}, u32[]{:S(2)}) collective-permute-start(bf16[256,256]{1,0:T(8,128)(2,1)S(1)} %bitcast.9), channel_id=1, source_target_pairs={{0,96},{32,0},{64,32},{96,64},{1,97},{33,1},{65,33},{97,65},{2,98}... | collective-permute-start | bytes 393224 | tf_op jit(solution)/shard_map/ppermute | solution.py:230
  59.7 4.0 %collective-permute-start.12 = (bf16[256,256]{1,0:T(8,128)(2,1)S(1)}, bf16[256,256]{1,0:T(8,128)(2,1)S(1)}, u32[]{:S(2)}, u32[]{:S(2)}) collective-permute-start(bf16[256,256]{1,0:T(8,128)(2,1)S(1)} %bitcast.11), channel_id=1, source_target_pairs={{0,1},{1,0},{2,3},{3,2},{4,5},{5,4},{6,7},{7,6},{8,9},{9,8},{10,11... | collective-permute-start | bytes 393224 | tf_op jit(solution)/shard_map/ppermute | solution.py:232
  63.7 3.1 %collective-permute-start.21 = (bf16[512,256]{1,0:T(8,128)(2,1)S(1)}, bf16[512,256]{1,0:T(8,128)(2,1)S(1)}, u32[]{:S(2)}, u32[]{:S(2)}) collective-permute-start(bf16[512,256]{1,0:T(8,128)(2,1)S(1)} %collective-permute-done.20.refs_1_), channel_id=1, source_target_pairs={{0,2},{1,31},{2,4},{3,1},{4,6},{5,3},{6,8},{7,5},{8,10},{9,7},{10,... | collective-permute-start | bytes 786440 | tf_op jit(solution)/shard_map/ppermute | solution.py:239
  67.1 2.5 %collective-permute-start.14 = (bf16[256,256]{1,0:T(8,128)(2,1)S(1)}, bf16[256,256]{1,0:T(8,128)(2,1)S(1)}, u32[]{:S(2)}, u32[]{:S(2)}) collective-permute-start(bf16[256,256]{1,0:T(8,128)(2,1)S(1)} %collective-permute-done.10.refs_2_), channel_id=1, source_target_pairs={{0,1},{1,0},{2,3},{3,2},{4,5},{5,4},{6,7},{7,6},{8,9},{9,8},{10,11... | collective-permute-start | bytes 393224 | tf_op jit(solution)/shard_map/ppermute | solution.py:232
  69.6 3.1 %collective-permute-start.6 = (bf16[512,256]{1,0:T(8,128)(2,1)S(1)}, bf16[512,256]{1,0:T(8,128)(2,1)S(1)}, u32[]{:S(2)}, u32[]{:S(2)}) collective-permute-start(bf16[512,256]{1,0:T(8,128)(2,1)S(1)} %collective-permute-done.5.refs_0_), channel_id=1, source_target_pairs={{0,2},{1,31},{2,4},{3,1},{4,6},{5,3},{6,8},{7,5},{8,10},{9,7},{10,... | collective-permute-start | bytes 786440 | tf_op jit(solution)/shard_map/ppermute | solution.py:238
  74.2 4.4 %fold.9 = (f32[2,128,2048]{2,1,0:T(8,128)S(1)}, f32[2,8,2048]{2,1,0:T(8,128)S(1)}) custom-call(bf16[512,256]{1,0:T(8,128)(2,1)S(1)} %bitcast.15, bf16[512,256]{1,0:T(8,128)(2,1)S(1)} %collective-permute-done.refs_1_, bf16[512,256]{1,0:T(8,128)(2,1)S(1)} %collective-permute-done.17.refs_2_, bf16[2,2048,128]{2,1,0:T(8,128)(2,1)S(1)} %lay.1.refs_3_.refs_2_.refs_1_), custom_call_target="tpu_custom_call" | custom-call | flops 1610612736 | tf_op jit(solution)/shard_map/fold/pallas_call | solution.py:83
  78.7 3.3 %fold.10 = (f32[2,128,2048]{2,1,0:T(8,128)S(1)}, f32[2,8,2048]{2,1,0:T(8,128)S(1)}) custom-call(bf16[512,256]{1,0:T(8,128)(2,1)S(1)} %collective-permute-done.1.refs_0_, bf16[512,256]{1,0:T(8,128)(2,1)S(1)} %collective-permute-done.18.refs_1_, bf16[2,2048,128]{2,1,0:T(8,128)(2,1)S(1)} %lay.1.refs_3_.refs_2_.refs_1_, ...), custom_call_target="tpu_custom_call", output_to_operand_aliasing={{0}: (3, {}), {1}: (4, {})} | custom-call | flops 1073741824 | tf_op jit(solution)/shard_map/fold/pallas_call | solution.py:83
  82.1 3.2 %fold.11 = (f32[2,128,2048]{2,1,0:T(8,128)S(1)}, f32[2,8,2048]{2,1,0:T(8,128)S(1)}) custom-call(bf16[512,256]{1,0:T(8,128)(2,1)S(1)} %collective-permute-done.2.refs_0_, bf16[512,256]{1,0:T(8,128)(2,1)S(1)} %collective-permute-done.19.refs_1_, bf16[2,2048,128]{2,1,0:T(8,128)(2,1)S(1)} %lay.1.refs_3_.refs_2_.refs_1_, ...), custom_call_target="tpu_custom_call", output_to_operand_aliasing={{0}: (3, {}), {1}: (4, {})} | custom-call | flops 1073741824 | tf_op jit(solution)/shard_map/fold/pallas_call | solution.py:83
  85.5 3.2 %fold.12 = (f32[2,128,2048]{2,1,0:T(8,128)S(1)}, f32[2,8,2048]{2,1,0:T(8,128)S(1)}) custom-call(bf16[512,256]{1,0:T(8,128)(2,1)S(1)} %collective-permute-done.3.refs_0_, bf16[512,256]{1,0:T(8,128)(2,1)S(1)} %collective-permute-done.20.refs_1_, bf16[2,2048,128]{2,1,0:T(8,128)(2,1)S(1)} %lay.1.refs_3_.refs_2_.refs_1_, ...), custom_call_target="tpu_custom_call", output_to_operand_aliasing={{0}: (3, {}), {1}: (4, {})} | custom-call | flops 1073741824 | tf_op jit(solution)/shard_map/fold/pallas_call | solution.py:83
  88.7 3.3 %fold.13 = (f32[2,128,2048]{2,1,0:T(8,128)S(1)}, f32[2,8,2048]{2,1,0:T(8,128)S(1)}) custom-call(bf16[512,256]{1,0:T(8,128)(2,1)S(1)} %collective-permute-done.4.refs_0_, bf16[512,256]{1,0:T(8,128)(2,1)S(1)} %collective-permute-done.21.refs_1_, bf16[2,2048,128]{2,1,0:T(8,128)(2,1)S(1)} %lay.1.refs_3_.refs_2_.refs_1_, ...), custom_call_target="tpu_custom_call", output_to_operand_aliasing={{0}: (3, {}), {1}: (4, {})} | custom-call | flops 1073741824 | tf_op jit(solution)/shard_map/fold/pallas_call | solution.py:83
  92.4 3.2 %fold.14 = (f32[2,128,2048]{2,1,0:T(8,128)S(1)}, f32[2,8,2048]{2,1,0:T(8,128)S(1)}) custom-call(bf16[512,256]{1,0:T(8,128)(2,1)S(1)} %collective-permute-done.5.refs_0_, bf16[512,256]{1,0:T(8,128)(2,1)S(1)} %collective-permute-done.22.refs_1_, bf16[2,2048,128]{2,1,0:T(8,128)(2,1)S(1)} %lay.1.refs_3_.refs_2_.refs_1_, ...), custom_call_target="tpu_custom_call", output_to_operand_aliasing={{0}: (3, {}), {1}: (4, {})} | custom-call | flops 1073741824 | tf_op jit(solution)/shard_map/fold/pallas_call | solution.py:83
  95.6 3.3 %fold.15 = (f32[2,128,2048]{2,1,0:T(8,128)S(1)}, f32[2,8,2048]{2,1,0:T(8,128)S(1)}) custom-call(bf16[512,256]{1,0:T(8,128)(2,1)S(1)} %collective-permute-done.6.refs_0_, bf16[512,256]{1,0:T(8,128)(2,1)S(1)} %collective-permute-done.23.refs_1_, bf16[2,2048,128]{2,1,0:T(8,128)(2,1)S(1)} %lay.1.refs_3_.refs_2_.refs_1_, ...), custom_call_target="tpu_custom_call", output_to_operand_aliasing={{0}: (3, {}), {1}: (4, {})} | custom-call | flops 1073741824 | tf_op jit(solution)/shard_map/fold/pallas_call | solution.py:83
  106.3 1.8 %collective-permute-done.28.refs_1_ = bf16[272,256]{1,0:T(8,128)(2,1)S(1)} collective-permute-done((bf16[272,256]{1,0:T(8,128)(2,1)S(1)}, bf16[272,256]{1,0:T(8,128)(2,1)S(1)}, u32[]{:S(2)}, u32[]{:S(2)}) %collective-permute-start.28) | collective-permute-done | bytes 139296 | tf_op jit(solution)/shard_map/ppermute | solution.py:250
  108.2 2.7 %collective-permute-done.29.refs_2_ = bf16[272,256]{1,0:T(8,128)(2,1)S(1)} collective-permute-done((bf16[272,256]{1,0:T(8,128)(2,1)S(1)}, bf16[272,256]{1,0:T(8,128)(2,1)S(1)}, u32[]{:S(2)}, u32[]{:S(2)}) %collective-permute-start.29) | collective-permute-done | bytes 139296 | tf_op jit(solution)/shard_map/ppermute | solution.py:250
  (54 shorter events, 18.5 us)
Async XLA Ops:
  1.4 26.3 %collective-permute-start = (bf16[512,256]{1,0:T(8,128)(2,1)S(1)}, bf16[512,256]{1,0:T(8,128)(2,1)S(1)}, u32[]{:S(2)}, u32[]{:S(2)}) collective-permute-start(bf16[512,256]{1,0:T(8,128)(2,1)S(1)} %bitcast.13), channel_id=1, source_target_pairs={{0,2},{1,31},{2,4},{3,1},{4,6},{5,3},{6,8},{7,5},{8,10},{9,7},{10,... | collective-permute-start | bytes 786440 | tf_op jit(solution)/shard_map/ppermute | solution.py:224
  24.4 6.4 %collective-permute-start.16 = (bf16[512,256]{1,0:T(8,128)(2,1)S(1)}, bf16[512,256]{1,0:T(8,128)(2,1)S(1)}, u32[]{:S(2)}, u32[]{:S(2)}) collective-permute-start(bf16[512,256]{1,0:T(8,128)(2,1)S(1)} %bitcast.14), channel_id=1, source_target_pairs={{0,1},{1,0},{2,3},{3,2},{4,5},{5,4},{6,7},{7,6},{8,9},{9,8},{10,11... | collective-permute-start | bytes 786440 | tf_op jit(solution)/shard_map/ppermute | solution.py:225
  27.7 6.4 %collective-permute-start.1 = (bf16[512,256]{1,0:T(8,128)(2,1)S(1)}, bf16[512,256]{1,0:T(8,128)(2,1)S(1)}, u32[]{:S(2)}, u32[]{:S(2)}) collective-permute-start(bf16[512,256]{1,0:T(8,128)(2,1)S(1)} %collective-permute-done.refs_1_), channel_id=1, source_target_pairs={{0,2},{1,31},{2,4},{3,1},{4,6},{5,3},{6,8},{7,5},{8,10},{9,7},{10,... | collective-permute-start | bytes 786440 | tf_op jit(solution)/shard_map/ppermute | solution.py:238
  30.8 6.4 %collective-permute-start.17 = (bf16[512,256]{1,0:T(8,128)(2,1)S(1)}, bf16[512,256]{1,0:T(8,128)(2,1)S(1)}, u32[]{:S(2)}, u32[]{:S(2)}) collective-permute-start(bf16[512,256]{1,0:T(8,128)(2,1)S(1)} %collective-permute-done.16), channel_id=1, source_target_pairs={{0,2},{1,31},{2,4},{3,1},{4,6},{5,3},{6,8},{7,5},{8,10},{9,7},{10,... | collective-permute-start | bytes 786440 | tf_op jit(solution)/shard_map/ppermute | solution.py:226
  34.1 6.4 %collective-permute-start.2 = (bf16[512,256]{1,0:T(8,128)(2,1)S(1)}, bf16[512,256]{1,0:T(8,128)(2,1)S(1)}, u32[]{:S(2)}, u32[]{:S(2)}) collective-permute-start(bf16[512,256]{1,0:T(8,128)(2,1)S(1)} %collective-permute-done.1.refs_0_), channel_id=1, source_target_pairs={{0,2},{1,31},{2,4},{3,1},{4,6},{5,3},{6,8},{7,5},{8,10},{9,7},{10,... | collective-permute-start | bytes 786440 | tf_op jit(solution)/shard_map/ppermute | solution.py:238
  37.3 6.4 %collective-permute-start.18 = (bf16[512,256]{1,0:T(8,128)(2,1)S(1)}, bf16[512,256]{1,0:T(8,128)(2,1)S(1)}, u32[]{:S(2)}, u32[]{:S(2)}) collective-permute-start(bf16[512,256]{1,0:T(8,128)(2,1)S(1)} %collective-permute-done.17.refs_2_), channel_id=1, source_target_pairs={{0,2},{1,31},{2,4},{3,1},{4,6},{5,3},{6,8},{7,5},{8,10},{9,7},{10,... | collective-permute-start | bytes 786440 | tf_op jit(solution)/shard_map/ppermute | solution.py:239
  40.6 6.4 %collective-permute-start.3 = (bf16[512,256]{1,0:T(8,128)(2,1)S(1)}, bf16[512,256]{1,0:T(8,128)(2,1)S(1)}, u32[]{:S(2)}, u32[]{:S(2)}) collective-permute-start(bf16[512,256]{1,0:T(8,128)(2,1)S(1)} %collective-permute-done.2.refs_0_), channel_id=1, source_target_pairs={{0,2},{1,31},{2,4},{3,1},{4,6},{5,3},{6,8},{7,5},{8,10},{9,7},{10,... | collective-permute-start | bytes 786440 | tf_op jit(solution)/shard_map/ppermute | solution.py:238
  43.7 6.4 %collective-permute-start.19 = (bf16[512,256]{1,0:T(8,128)(2,1)S(1)}, bf16[512,256]{1,0:T(8,128)(2,1)S(1)}, u32[]{:S(2)}, u32[]{:S(2)}) collective-permute-start(bf16[512,256]{1,0:T(8,128)(2,1)S(1)} %collective-permute-done.18.refs_1_), channel_id=1, source_target_pairs={{0,2},{1,31},{2,4},{3,1},{4,6},{5,3},{6,8},{7,5},{8,10},{9,7},{10,... | collective-permute-start | bytes 786440 | tf_op jit(solution)/shard_map/ppermute | solution.py:239
  47.0 8.3 %collective-permute-start.4 = (bf16[512,256]{1,0:T(8,128)(2,1)S(1)}, bf16[512,256]{1,0:T(8,128)(2,1)S(1)}, u32[]{:S(2)}, u32[]{:S(2)}) collective-permute-start(bf16[512,256]{1,0:T(8,128)(2,1)S(1)} %collective-permute-done.3.refs_0_), channel_id=1, source_target_pairs={{0,2},{1,31},{2,4},{3,1},{4,6},{5,3},{6,8},{7,5},{8,10},{9,7},{10,... | collective-permute-start | bytes 786440 | tf_op jit(solution)/shard_map/ppermute | solution.py:238
  50.1 13.6 %collective-permute-start.20 = (bf16[512,256]{1,0:T(8,128)(2,1)S(1)}, bf16[512,256]{1,0:T(8,128)(2,1)S(1)}, u32[]{:S(2)}, u32[]{:S(2)}) collective-permute-start(bf16[512,256]{1,0:T(8,128)(2,1)S(1)} %collective-permute-done.19.refs_1_), channel_id=1, source_target_pairs={{0,2},{1,31},{2,4},{3,1},{4,6},{5,3},{6,8},{7,5},{8,10},{9,7},{10,... | collective-permute-start | bytes 786440 | tf_op jit(solution)/shard_map/ppermute | solution.py:239
  53.9 5.8 %collective-permute-start.9 = (bf16[256,256]{1,0:T(8,128)(2,1)S(1)}, bf16[256,256]{1,0:T(8,128)(2,1)S(1)}, u32[]{:S(2)}, u32[]{:S(2)}) collective-permute-start(bf16[256,256]{1,0:T(8,128)(2,1)S(1)} %bitcast.8), channel_id=1, source_target_pairs={{0,32},{32,64},{64,96},{96,0},{1,33},{33,65},{65,97},{97,1},{2,34}... | collective-permute-start | bytes 393224 | tf_op jit(solution)/shard_map/ppermute | solution.py:230
  55.3 14.3 %collective-permute-start.5 = (bf16[512,256]{1,0:T(8,128)(2,1)S(1)}, bf16[512,256]{1,0:T(8,128)(2,1)S(1)}, u32[]{:S(2)}, u32[]{:S(2)}) collective-permute-start(bf16[512,256]{1,0:T(8,128)(2,1)S(1)} %collective-permute-done.4.refs_0_), channel_id=1, source_target_pairs={{0,2},{1,31},{2,4},{3,1},{4,6},{5,3},{6,8},{7,5},{8,10},{9,7},{10,... | collective-permute-start | bytes 786440 | tf_op jit(solution)/shard_map/ppermute | solution.py:238
  56.6 10.2 %collective-permute-start.10 = (bf16[256,256]{1,0:T(8,128)(2,1)S(1)}, bf16[256,256]{1,0:T(8,128)(2,1)S(1)}, u32[]{:S(2)}, u32[]{:S(2)}) collective-permute-start(bf16[256,256]{1,0:T(8,128)(2,1)S(1)} %bitcast.9), channel_id=1, source_target_pairs={{0,96},{32,0},{64,32},{96,64},{1,97},{33,1},{65,33},{97,65},{2,98}... | collective-permute-start | bytes 393224 | tf_op jit(solution)/shard_map/ppermute | solution.py:230
  59.4 7.6 %collective-permute-start.11 = (bf16[256,256]{1,0:T(8,128)(2,1)S(1)}, bf16[256,256]{1,0:T(8,128)(2,1)S(1)}, u32[]{:S(2)}, u32[]{:S(2)}) collective-permute-start(bf16[256,256]{1,0:T(8,128)(2,1)S(1)} %bitcast.10), channel_id=1, source_target_pairs={{0,64},{32,96},{64,0},{96,32},{1,65},{33,97},{65,1},{97,33},{2,66}... | collective-permute-start | bytes 393224 | tf_op jit(solution)/shard_map/ppermute | solution.py:230
  59.7 9.9 %collective-permute-start.12 = (bf16[256,256]{1,0:T(8,128)(2,1)S(1)}, bf16[256,256]{1,0:T(8,128)(2,1)S(1)}, u32[]{:S(2)}, u32[]{:S(2)}) collective-permute-start(bf16[256,256]{1,0:T(8,128)(2,1)S(1)} %bitcast.11), channel_id=1, source_target_pairs={{0,1},{1,0},{2,3},{3,2},{4,5},{5,4},{6,7},{7,6},{8,9},{9,8},{10,11... | collective-permute-start | bytes 393224 | tf_op jit(solution)/shard_map/ppermute | solution.py:232
  63.7 9.2 %collective-permute-start.21 = (bf16[512,256]{1,0:T(8,128)(2,1)S(1)}, bf16[512,256]{1,0:T(8,128)(2,1)S(1)}, u32[]{:S(2)}, u32[]{:S(2)}) collective-permute-start(bf16[512,256]{1,0:T(8,128)(2,1)S(1)} %collective-permute-done.20.refs_1_), channel_id=1, source_target_pairs={{0,2},{1,31},{2,4},{3,1},{4,6},{5,3},{6,8},{7,5},{8,10},{9,7},{10,... | collective-permute-start | bytes 786440 | tf_op jit(solution)/shard_map/ppermute | solution.py:239
  66.8 5.9 %collective-permute-start.13 = (bf16[256,256]{1,0:T(8,128)(2,1)S(1)}, bf16[256,256]{1,0:T(8,128)(2,1)S(1)}, u32[]{:S(2)}, u32[]{:S(2)}) collective-permute-start(bf16[256,256]{1,0:T(8,128)(2,1)S(1)} %collective-permute-done.9.refs_1_), channel_id=1, source_target_pairs={{0,1},{1,0},{2,3},{3,2},{4,5},{5,4},{6,7},{7,6},{8,9},{9,8},{10,11... | collective-permute-start | bytes 393224 | tf_op jit(solution)/shard_map/ppermute | solution.py:232
  69.6 12.3 %collective-permute-start.6 = (bf16[512,256]{1,0:T(8,128)(2,1)S(1)}, bf16[512,256]{1,0:T(8,128)(2,1)S(1)}, u32[]{:S(2)}, u32[]{:S(2)}) collective-permute-start(bf16[512,256]{1,0:T(8,128)(2,1)S(1)} %collective-permute-done.5.refs_0_), channel_id=1, source_target_pairs={{0,2},{1,31},{2,4},{3,1},{4,6},{5,3},{6,8},{7,5},{8,10},{9,7},{10,... | collective-permute-start | bytes 786440 | tf_op jit(solution)/shard_map/ppermute | solution.py:238
  72.9 12.4 %collective-permute-start.22 = (bf16[512,256]{1,0:T(8,128)(2,1)S(1)}, bf16[512,256]{1,0:T(8,128)(2,1)S(1)}, u32[]{:S(2)}, u32[]{:S(2)}) collective-permute-start(bf16[512,256]{1,0:T(8,128)(2,1)S(1)} %collective-permute-done.21.refs_1_), channel_id=1, source_target_pairs={{0,2},{1,31},{2,4},{3,1},{4,6},{5,3},{6,8},{7,5},{8,10},{9,7},{10,... | collective-permute-start | bytes 786440 | tf_op jit(solution)/shard_map/ppermute | solution.py:239
  81.9 10.0 %collective-permute-start.7 = (bf16[512,256]{1,0:T(8,128)(2,1)S(1)}, bf16[512,256]{1,0:T(8,128)(2,1)S(1)}, u32[]{:S(2)}, u32[]{:S(2)}) collective-permute-start(bf16[512,256]{1,0:T(8,128)(2,1)S(1)} %collective-permute-done.6.refs_0_), channel_id=1, source_target_pairs={{0,2},{1,31},{2,4},{3,1},{4,6},{5,3},{6,8},{7,5},{8,10},{9,7},{10,... | collective-permute-start | bytes 786440 | tf_op jit(solution)/shard_map/ppermute | solution.py:243
  85.3 10.3 %collective-permute-start.23 = (bf16[512,256]{1,0:T(8,128)(2,1)S(1)}, bf16[512,256]{1,0:T(8,128)(2,1)S(1)}, u32[]{:S(2)}, u32[]{:S(2)}) collective-permute-start(bf16[512,256]{1,0:T(8,128)(2,1)S(1)} %collective-permute-done.22.refs_1_), channel_id=1, source_target_pairs={{0,2},{1,31},{2,4},{3,1},{4,6},{5,3},{6,8},{7,5},{8,10},{9,7},{10,... | collective-permute-start | bytes 786440 | tf_op jit(solution)/shard_map/ppermute | solution.py:239
  92.0 9.6 %collective-permute-start.8 = (bf16[512,256]{1,0:T(8,128)(2,1)S(1)}, bf16[512,256]{1,0:T(8,128)(2,1)S(1)}, u32[]{:S(2)}, u32[]{:S(2)}) collective-permute-start(bf16[512,256]{1,0:T(8,128)(2,1)S(1)} %collective-permute-done.7.refs_0_), channel_id=1, source_target_pairs={{0,1},{1,0},{2,3},{3,2},{4,5},{5,4},{6,7},{7,6},{8,9},{9,8},{10,11... | collective-permute-start | bytes 786440 | tf_op jit(solution)/shard_map/ppermute | solution.py:244
  104.3 6.5 %collective-permute-start.29 = (bf16[272,256]{1,0:T(8,128)(2,1)S(1)}, bf16[272,256]{1,0:T(8,128)(2,1)S(1)}, u32[]{:S(2)}, u32[]{:S(2)}) collective-permute-start(bf16[272,256]{1,0:T(8,128)(2,1)S(1)} %get-tuple-element.57), channel_id=1, source_target_pairs={{0,32},{32,64},{64,96},{96,0},{1,33},{33,65},{65,97},{97,1},{2,34}... | collective-permute-start | bytes 417800 | tf_op jit(solution)/shard_map/ppermute | solution.py:250
  104.8 7.7 %collective-permute-start.30 = (bf16[272,256]{1,0:T(8,128)(2,1)S(1)}, bf16[272,256]{1,0:T(8,128)(2,1)S(1)}, u32[]{:S(2)}, u32[]{:S(2)}) collective-permute-start(bf16[272,256]{1,0:T(8,128)(2,1)S(1)} %get-tuple-element.58), channel_id=1, source_target_pairs={{0,64},{32,96},{64,0},{96,32},{1,65},{33,97},{65,1},{97,33},{2,66}... | collective-permute-start | bytes 417800 | tf_op jit(solution)/shard_map/ppermute | solution.py:250
  (7 other events, 26.8 us)

commit v3 on v2

--- a/solution.py
+++ b/solution.py
@@ -246,11 +246,10 @@
     mine = fold(mine, [other], q_all, share)
 
     parts = pack(mine, heads, own, more=sent)
-    parts = [parts[0]] + [
-        lax.ppermute(a, "x", [(x, (x - d) % n_x) for x in range(n_x)])
-        for d, a in zip(offsets[1:], parts[1:])
-    ]
-    return merge(parts, heads, width)
+    home = [parts[0]]
+    for d, part in zip(offsets[1:], parts[1:]):
+        home.append(lax.ppermute(part, "x", [(x, (x - d) % n_x) for x in range(n_x)]))
+    return merge(home, heads, width)
 
 
 def solution(mesh):

time: 114 us -> 114 us (level)
  no operation moved by 1% of the time
where the time goes in v3:
time: 114 us; the launch traced here: 113 us
  starting transfers between devices  69.1 us (61%)
  Pallas kernels  27.9 us (24%)
  waiting for transfers between devices  13.8 us (12%)
  other arithmetic  1.31 us (1%)
    pallas_call x9, Pallas kernels, fold(): pl.pallas_call(functools.partial(fold_kernel, pieces=pieces, heads=heads,...  26.5 us
    ppermute x1, starting transfers between devices, body(): ahead = forward(here)  23 us
    ppermute x6, starting transfers between devices, body(): near = forward(chunk[0])  16.8 us
    ppermute x6, starting transfers between devices, body(): chunk = [near, forward(chunk[1])]  13 us
    ppermute x4, starting transfers between devices, body(): q_theirs = [swap(a) for a in q_mine]  6.81 us
    ppermute x3, waiting for transfers between devices, body(): lax.ppermute(part, 'x', [(x, (x - d) % n_x) for x in range(n_x)])  6.1 us
    ppermute x3, starting transfers between devices, body(): lax.ppermute(q, 'x', [(x, (x + d) % n_x) for x in range(n_x)])  4.59 us
    ppermute x6, waiting for transfers between devices, body(): near = forward(chunk[0])  4.32 us
  transfers between devices with their start and end apart: 31, of which 7 were waited for; matrix products, arithmetic and copies ran while one was open for 1% of the time, Pallas kernels for 24%

profile of v3, /device:TPU:33, one launch (start us, length us, event | category | flops | bytes accessed | tf_op | source)
XLA Modules:
  0.0 113.3 jit_solution(12197904555176267430)
XLA Ops:
  1.4 23.0 %collective-permute-start = (bf16[512,256]{1,0:T(8,128)(2,1)S(1)}, bf16[512,256]{1,0:T(8,128)(2,1)S(1)}, u32[]{:S(2)}, u32[]{:S(2)}) collective-permute-start(bf16[512,256]{1,0:T(8,128)(2,1)S(1)} %bitcast.13), channel_id=1, source_target_pairs={{0,2},{1,31},{2,4},{3,1},{4,6},{5,3},{6,8},{7,5},{8,10},{9,7},{10,... | collective-permute-start | bytes 786440 | tf_op jit(solution)/shard_map/ppermute | solution.py:224
  24.4 3.3 %collective-permute-done.refs_1_ = bf16[512,256]{1,0:T(8,128)(2,1)S(1)} collective-permute-done((bf16[512,256]{1,0:T(8,128)(2,1)S(1)}, bf16[512,256]{1,0:T(8,128)(2,1)S(1)}, u32[]{:S(2)}, u32[]{:S(2)}) %collective-permute-start) | collective-permute-done | bytes 262176 | tf_op jit(solution)/shard_map/ppermute | solution.py:224
  27.7 3.1 %collective-permute-start.1 = (bf16[512,256]{1,0:T(8,128)(2,1)S(1)}, bf16[512,256]{1,0:T(8,128)(2,1)S(1)}, u32[]{:S(2)}, u32[]{:S(2)}) collective-permute-start(bf16[512,256]{1,0:T(8,128)(2,1)S(1)} %collective-permute-done.refs_1_), channel_id=1, source_target_pairs={{0,2},{1,31},{2,4},{3,1},{4,6},{5,3},{6,8},{7,5},{8,10},{9,7},{10,... | collective-permute-start | bytes 786440 | tf_op jit(solution)/shard_map/ppermute | solution.py:238
  30.8 3.3 %collective-permute-done.1.refs_0_ = bf16[512,256]{1,0:T(8,128)(2,1)S(1)} collective-permute-done((bf16[512,256]{1,0:T(8,128)(2,1)S(1)}, bf16[512,256]{1,0:T(8,128)(2,1)S(1)}, u32[]{:S(2)}, u32[]{:S(2)}) %collective-permute-start.1) | collective-permute-done | bytes 262176 | tf_op jit(solution)/shard_map/ppermute | solution.py:238
  34.1 3.1 %collective-permute-start.2 = (bf16[512,256]{1,0:T(8,128)(2,1)S(1)}, bf16[512,256]{1,0:T(8,128)(2,1)S(1)}, u32[]{:S(2)}, u32[]{:S(2)}) collective-permute-start(bf16[512,256]{1,0:T(8,128)(2,1)S(1)} %collective-permute-done.1.refs_0_), channel_id=1, source_target_pairs={{0,2},{1,31},{2,4},{3,1},{4,6},{5,3},{6,8},{7,5},{8,10},{9,7},{10,... | collective-permute-start | bytes 786440 | tf_op jit(solution)/shard_map/ppermute | solution.py:238
  37.3 2.8 %collective-permute-start.18 = (bf16[512,256]{1,0:T(8,128)(2,1)S(1)}, bf16[512,256]{1,0:T(8,128)(2,1)S(1)}, u32[]{:S(2)}, u32[]{:S(2)}) collective-permute-start(bf16[512,256]{1,0:T(8,128)(2,1)S(1)} %collective-permute-done.17.refs_2_), channel_id=1, source_target_pairs={{0,2},{1,31},{2,4},{3,1},{4,6},{5,3},{6,8},{7,5},{8,10},{9,7},{10,... | collective-permute-start | bytes 786440 | tf_op jit(solution)/shard_map/ppermute | solution.py:239
  40.6 3.1 %collective-permute-start.3 = (bf16[512,256]{1,0:T(8,128)(2,1)S(1)}, bf16[512,256]{1,0:T(8,128)(2,1)S(1)}, u32[]{:S(2)}, u32[]{:S(2)}) collective-permute-start(bf16[512,256]{1,0:T(8,128)(2,1)S(1)} %collective-permute-done.2.refs_0_), channel_id=1, source_target_pairs={{0,2},{1,31},{2,4},{3,1},{4,6},{5,3},{6,8},{7,5},{8,10},{9,7},{10,... | collective-permute-start | bytes 786440 | tf_op jit(solution)/shard_map/ppermute | solution.py:238
  43.7 2.8 %collective-permute-start.19 = (bf16[512,256]{1,0:T(8,128)(2,1)S(1)}, bf16[512,256]{1,0:T(8,128)(2,1)S(1)}, u32[]{:S(2)}, u32[]{:S(2)}) collective-permute-start(bf16[512,256]{1,0:T(8,128)(2,1)S(1)} %collective-permute-done.18.refs_1_), channel_id=1, source_target_pairs={{0,2},{1,31},{2,4},{3,1},{4,6},{5,3},{6,8},{7,5},{8,10},{9,7},{10,... | collective-permute-start | bytes 786440 | tf_op jit(solution)/shard_map/ppermute | solution.py:239
  47.0 3.1 %collective-permute-start.4 = (bf16[512,256]{1,0:T(8,128)(2,1)S(1)}, bf16[512,256]{1,0:T(8,128)(2,1)S(1)}, u32[]{:S(2)}, u32[]{:S(2)}) collective-permute-start(bf16[512,256]{1,0:T(8,128)(2,1)S(1)} %collective-permute-done.3.refs_0_), channel_id=1, source_target_pairs={{0,2},{1,31},{2,4},{3,1},{4,6},{5,3},{6,8},{7,5},{8,10},{9,7},{10,... | collective-permute-start | bytes 786440 | tf_op jit(solution)/shard_map/ppermute | solution.py:238
  50.1 2.8 %collective-permute-start.20 = (bf16[512,256]{1,0:T(8,128)(2,1)S(1)}, bf16[512,256]{1,0:T(8,128)(2,1)S(1)}, u32[]{:S(2)}, u32[]{:S(2)}) collective-permute-start(bf16[512,256]{1,0:T(8,128)(2,1)S(1)} %collective-permute-done.19.refs_1_), channel_id=1, source_target_pairs={{0,2},{1,31},{2,4},{3,1},{4,6},{5,3},{6,8},{7,5},{8,10},{9,7},{10,... | collective-permute-start | bytes 786440 | tf_op jit(solution)/shard_map/ppermute | solution.py:239
  56.6 2.9 %collective-permute-start.10 = (bf16[256,256]{1,0:T(8,128)(2,1)S(1)}, bf16[256,256]{1,0:T(8,128)(2,1)S(1)}, u32[]{:S(2)}, u32[]{:S(2)}) collective-permute-start(bf16[256,256]{1,0:T(8,128)(2,1)S(1)} %bitcast.9), channel_id=1, source_target_pairs={{0,96},{32,0},{64,32},{96,64},{1,97},{33,1},{65,33},{97,65},{2,98}... | collective-permute-start | bytes 393224 | tf_op jit(solution)/shard_map/ppermute | solution.py:230
  59.7 4.0 %collective-permute-start.12 = (bf16[256,256]{1,0:T(8,128)(2,1)S(1)}, bf16[256,256]{1,0:T(8,128)(2,1)S(1)}, u32[]{:S(2)}, u32[]{:S(2)}) collective-permute-start(bf16[256,256]{1,0:T(8,128)(2,1)S(1)} %bitcast.11), channel_id=1, source_target_pairs={{0,1},{1,0},{2,3},{3,2},{4,5},{5,4},{6,7},{7,6},{8,9},{9,8},{10,11... | collective-permute-start | bytes 393224 | tf_op jit(solution)/shard_map/ppermute | solution.py:232
  63.7 3.1 %collective-permute-start.21 = (bf16[512,256]{1,0:T(8,128)(2,1)S(1)}, bf16[512,256]{1,0:T(8,128)(2,1)S(1)}, u32[]{:S(2)}, u32[]{:S(2)}) collective-permute-start(bf16[512,256]{1,0:T(8,128)(2,1)S(1)} %collective-permute-done.20.refs_1_), channel_id=1, source_target_pairs={{0,2},{1,31},{2,4},{3,1},{4,6},{5,3},{6,8},{7,5},{8,10},{9,7},{10,... | collective-permute-start | bytes 786440 | tf_op jit(solution)/shard_map/ppermute | solution.py:239
  67.1 2.5 %collective-permute-start.14 = (bf16[256,256]{1,0:T(8,128)(2,1)S(1)}, bf16[256,256]{1,0:T(8,128)(2,1)S(1)}, u32[]{:S(2)}, u32[]{:S(2)}) collective-permute-start(bf16[256,256]{1,0:T(8,128)(2,1)S(1)} %collective-permute-done.10.refs_2_), channel_id=1, source_target_pairs={{0,1},{1,0},{2,3},{3,2},{4,5},{5,4},{6,7},{7,6},{8,9},{9,8},{10,11... | collective-permute-start | bytes 393224 | tf_op jit(solution)/shard_map/ppermute | solution.py:232
  69.6 3.1 %collective-permute-start.6 = (bf16[512,256]{1,0:T(8,128)(2,1)S(1)}, bf16[512,256]{1,0:T(8,128)(2,1)S(1)}, u32[]{:S(2)}, u32[]{:S(2)}) collective-permute-start(bf16[512,256]{1,0:T(8,128)(2,1)S(1)} %collective-permute-done.5.refs_0_), channel_id=1, source_target_pairs={{0,2},{1,31},{2,4},{3,1},{4,6},{5,3},{6,8},{7,5},{8,10},{9,7},{10,... | collective-permute-start | bytes 786440 | tf_op jit(solution)/shard_map/ppermute | solution.py:238
  74.2 4.4 %fold.9 = (f32[2,128,2048]{2,1,0:T(8,128)S(1)}, f32[2,8,2048]{2,1,0:T(8,128)S(1)}) custom-call(bf16[512,256]{1,0:T(8,128)(2,1)S(1)} %bitcast.15, bf16[512,256]{1,0:T(8,128)(2,1)S(1)} %collective-permute-done.refs_1_, bf16[512,256]{1,0:T(8,128)(2,1)S(1)} %collective-permute-done.17.refs_2_, bf16[2,2048,128]{2,1,0:T(8,128)(2,1)S(1)} %lay.1.refs_3_.refs_2_.refs_1_), custom_call_target="tpu_custom_call" | custom-call | flops 1610612736 | tf_op jit(solution)/shard_map/fold/pallas_call | solution.py:83
  78.7 3.3 %fold.10 = (f32[2,128,2048]{2,1,0:T(8,128)S(1)}, f32[2,8,2048]{2,1,0:T(8,128)S(1)}) custom-call(bf16[512,256]{1,0:T(8,128)(2,1)S(1)} %collective-permute-done.1.refs_0_, bf16[512,256]{1,0:T(8,128)(2,1)S(1)} %collective-permute-done.18.refs_1_, bf16[2,2048,128]{2,1,0:T(8,128)(2,1)S(1)} %lay.1.refs_3_.refs_2_.refs_1_, ...), custom_call_target="tpu_custom_call", output_to_operand_aliasing={{0}: (3, {}), {1}: (4, {})} | custom-call | flops 1073741824 | tf_op jit(solution)/shard_map/fold/pallas_call | solution.py:83
  82.1 3.2 %fold.11 = (f32[2,128,2048]{2,1,0:T(8,128)S(1)}, f32[2,8,2048]{2,1,0:T(8,128)S(1)}) custom-call(bf16[512,256]{1,0:T(8,128)(2,1)S(1)} %collective-permute-done.2.refs_0_, bf16[512,256]{1,0:T(8,128)(2,1)S(1)} %collective-permute-done.19.refs_1_, bf16[2,2048,128]{2,1,0:T(8,128)(2,1)S(1)} %lay.1.refs_3_.refs_2_.refs_1_, ...), custom_call_target="tpu_custom_call", output_to_operand_aliasing={{0}: (3, {}), {1}: (4, {})} | custom-call | flops 1073741824 | tf_op jit(solution)/shard_map/fold/pallas_call | solution.py:83
  85.5 3.2 %fold.12 = (f32[2,128,2048]{2,1,0:T(8,128)S(1)}, f32[2,8,2048]{2,1,0:T(8,128)S(1)}) custom-call(bf16[512,256]{1,0:T(8,128)(2,1)S(1)} %collective-permute-done.3.refs_0_, bf16[512,256]{1,0:T(8,128)(2,1)S(1)} %collective-permute-done.20.refs_1_, bf16[2,2048,128]{2,1,0:T(8,128)(2,1)S(1)} %lay.1.refs_3_.refs_2_.refs_1_, ...), custom_call_target="tpu_custom_call", output_to_operand_aliasing={{0}: (3, {}), {1}: (4, {})} | custom-call | flops 1073741824 | tf_op jit(solution)/shard_map/fold/pallas_call | solution.py:83
  88.7 3.3 %fold.13 = (f32[2,128,2048]{2,1,0:T(8,128)S(1)}, f32[2,8,2048]{2,1,0:T(8,128)S(1)}) custom-call(bf16[512,256]{1,0:T(8,128)(2,1)S(1)} %collective-permute-done.4.refs_0_, bf16[512,256]{1,0:T(8,128)(2,1)S(1)} %collective-permute-done.21.refs_1_, bf16[2,2048,128]{2,1,0:T(8,128)(2,1)S(1)} %lay.1.refs_3_.refs_2_.refs_1_, ...), custom_call_target="tpu_custom_call", output_to_operand_aliasing={{0}: (3, {}), {1}: (4, {})} | custom-call | flops 1073741824 | tf_op jit(solution)/shard_map/fold/pallas_call | solution.py:83
  92.4 3.2 %fold.14 = (f32[2,128,2048]{2,1,0:T(8,128)S(1)}, f32[2,8,2048]{2,1,0:T(8,128)S(1)}) custom-call(bf16[512,256]{1,0:T(8,128)(2,1)S(1)} %collective-permute-done.5.refs_0_, bf16[512,256]{1,0:T(8,128)(2,1)S(1)} %collective-permute-done.22.refs_1_, bf16[2,2048,128]{2,1,0:T(8,128)(2,1)S(1)} %lay.1.refs_3_.refs_2_.refs_1_, ...), custom_call_target="tpu_custom_call", output_to_operand_aliasing={{0}: (3, {}), {1}: (4, {})} | custom-call | flops 1073741824 | tf_op jit(solution)/shard_map/fold/pallas_call | solution.py:83
  95.6 3.3 %fold.15 = (f32[2,128,2048]{2,1,0:T(8,128)S(1)}, f32[2,8,2048]{2,1,0:T(8,128)S(1)}) custom-call(bf16[512,256]{1,0:T(8,128)(2,1)S(1)} %collective-permute-done.6.refs_0_, bf16[512,256]{1,0:T(8,128)(2,1)S(1)} %collective-permute-done.23.refs_1_, bf16[2,2048,128]{2,1,0:T(8,128)(2,1)S(1)} %lay.1.refs_3_.refs_2_.refs_1_, ...), custom_call_target="tpu_custom_call", output_to_operand_aliasing={{0}: (3, {}), {1}: (4, {})} | custom-call | flops 1073741824 | tf_op jit(solution)/shard_map/fold/pallas_call | solution.py:83
  106.3 1.8 %collective-permute-done.28.refs_1_ = bf16[272,256]{1,0:T(8,128)(2,1)S(1)} collective-permute-done((bf16[272,256]{1,0:T(8,128)(2,1)S(1)}, bf16[272,256]{1,0:T(8,128)(2,1)S(1)}, u32[]{:S(2)}, u32[]{:S(2)}) %collective-permute-start.28) | collective-permute-done | bytes 139296 | tf_op jit(solution)/shard_map/ppermute | solution.py:251
  108.2 2.7 %collective-permute-done.29.refs_2_ = bf16[272,256]{1,0:T(8,128)(2,1)S(1)} collective-permute-done((bf16[272,256]{1,0:T(8,128)(2,1)S(1)}, bf16[272,256]{1,0:T(8,128)(2,1)S(1)}, u32[]{:S(2)}, u32[]{:S(2)}) %collective-permute-start.29) | collective-permute-done | bytes 139296 | tf_op jit(solution)/shard_map/ppermute | solution.py:251
  (54 shorter events, 18.5 us)
Async XLA Ops:
  1.4 26.3 %collective-permute-start = (bf16[512,256]{1,0:T(8,128)(2,1)S(1)}, bf16[512,256]{1,0:T(8,128)(2,1)S(1)}, u32[]{:S(2)}, u32[]{:S(2)}) collective-permute-start(bf16[512,256]{1,0:T(8,128)(2,1)S(1)} %bitcast.13), channel_id=1, source_target_pairs={{0,2},{1,31},{2,4},{3,1},{4,6},{5,3},{6,8},{7,5},{8,10},{9,7},{10,... | collective-permute-start | bytes 786440 | tf_op jit(solution)/shard_map/ppermute | solution.py:224
  24.4 6.4 %collective-permute-start.16 = (bf16[512,256]{1,0:T(8,128)(2,1)S(1)}, bf16[512,256]{1,0:T(8,128)(2,1)S(1)}, u32[]{:S(2)}, u32[]{:S(2)}) collective-permute-start(bf16[512,256]{1,0:T(8,128)(2,1)S(1)} %bitcast.14), channel_id=1, source_target_pairs={{0,1},{1,0},{2,3},{3,2},{4,5},{5,4},{6,7},{7,6},{8,9},{9,8},{10,11... | collective-permute-start | bytes 786440 | tf_op jit(solution)/shard_map/ppermute | solution.py:225
  27.7 6.4 %collective-permute-start.1 = (bf16[512,256]{1,0:T(8,128)(2,1)S(1)}, bf16[512,256]{1,0:T(8,128)(2,1)S(1)}, u32[]{:S(2)}, u32[]{:S(2)}) collective-permute-start(bf16[512,256]{1,0:T(8,128)(2,1)S(1)} %collective-permute-done.refs_1_), channel_id=1, source_target_pairs={{0,2},{1,31},{2,4},{3,1},{4,6},{5,3},{6,8},{7,5},{8,10},{9,7},{10,... | collective-permute-start | bytes 786440 | tf_op jit(solution)/shard_map/ppermute | solution.py:238
  30.8 6.4 %collective-permute-start.17 = (bf16[512,256]{1,0:T(8,128)(2,1)S(1)}, bf16[512,256]{1,0:T(8,128)(2,1)S(1)}, u32[]{:S(2)}, u32[]{:S(2)}) collective-permute-start(bf16[512,256]{1,0:T(8,128)(2,1)S(1)} %collective-permute-done.16), channel_id=1, source_target_pairs={{0,2},{1,31},{2,4},{3,1},{4,6},{5,3},{6,8},{7,5},{8,10},{9,7},{10,... | collective-permute-start | bytes 786440 | tf_op jit(solution)/shard_map/ppermute | solution.py:226
  34.1 6.4 %collective-permute-start.2 = (bf16[512,256]{1,0:T(8,128)(2,1)S(1)}, bf16[512,256]{1,0:T(8,128)(2,1)S(1)}, u32[]{:S(2)}, u32[]{:S(2)}) collective-permute-start(bf16[512,256]{1,0:T(8,128)(2,1)S(1)} %collective-permute-done.1.refs_0_), channel_id=1, source_target_pairs={{0,2},{1,31},{2,4},{3,1},{4,6},{5,3},{6,8},{7,5},{8,10},{9,7},{10,... | collective-permute-start | bytes 786440 | tf_op jit(solution)/shard_map/ppermute | solution.py:238
  37.3 6.4 %collective-permute-start.18 = (bf16[512,256]{1,0:T(8,128)(2,1)S(1)}, bf16[512,256]{1,0:T(8,128)(2,1)S(1)}, u32[]{:S(2)}, u32[]{:S(2)}) collective-permute-start(bf16[512,256]{1,0:T(8,128)(2,1)S(1)} %collective-permute-done.17.refs_2_), channel_id=1, source_target_pairs={{0,2},{1,31},{2,4},{3,1},{4,6},{5,3},{6,8},{7,5},{8,10},{9,7},{10,... | collective-permute-start | bytes 786440 | tf_op jit(solution)/shard_map/ppermute | solution.py:239
  40.6 6.4 %collective-permute-start.3 = (bf16[512,256]{1,0:T(8,128)(2,1)S(1)}, bf16[512,256]{1,0:T(8,128)(2,1)S(1)}, u32[]{:S(2)}, u32[]{:S(2)}) collective-permute-start(bf16[512,256]{1,0:T(8,128)(2,1)S(1)} %collective-permute-done.2.refs_0_), channel_id=1, source_target_pairs={{0,2},{1,31},{2,4},{3,1},{4,6},{5,3},{6,8},{7,5},{8,10},{9,7},{10,... | collective-permute-start | bytes 786440 | tf_op jit(solution)/shard_map/ppermute | solution.py:238
  43.7 6.4 %collective-permute-start.19 = (bf16[512,256]{1,0:T(8,128)(2,1)S(1)}, bf16[512,256]{1,0:T(8,128)(2,1)S(1)}, u32[]{:S(2)}, u32[]{:S(2)}) collective-permute-start(bf16[512,256]{1,0:T(8,128)(2,1)S(1)} %collective-permute-done.18.refs_1_), channel_id=1, source_target_pairs={{0,2},{1,31},{2,4},{3,1},{4,6},{5,3},{6,8},{7,5},{8,10},{9,7},{10,... | collective-permute-start | bytes 786440 | tf_op jit(solution)/shard_map/ppermute | solution.py:239
  47.0 8.3 %collective-permute-start.4 = (bf16[512,256]{1,0:T(8,128)(2,1)S(1)}, bf16[512,256]{1,0:T(8,128)(2,1)S(1)}, u32[]{:S(2)}, u32[]{:S(2)}) collective-permute-start(bf16[512,256]{1,0:T(8,128)(2,1)S(1)} %collective-permute-done.3.refs_0_), channel_id=1, source_target_pairs={{0,2},{1,31},{2,4},{3,1},{4,6},{5,3},{6,8},{7,5},{8,10},{9,7},{10,... | collective-permute-start | bytes 786440 | tf_op jit(solution)/shard_map/ppermute | solution.py:238
  50.1 13.6 %collective-permute-start.20 = (bf16[512,256]{1,0:T(8,128)(2,1)S(1)}, bf16[512,256]{1,0:T(8,128)(2,1)S(1)}, u32[]{:S(2)}, u32[]{:S(2)}) collective-permute-start(bf16[512,256]{1,0:T(8,128)(2,1)S(1)} %collective-permute-done.19.refs_1_), channel_id=1, source_target_pairs={{0,2},{1,31},{2,4},{3,1},{4,6},{5,3},{6,8},{7,5},{8,10},{9,7},{10,... | collective-permute-start | bytes 786440 | tf_op jit(solution)/shard_map/ppermute | solution.py:239
  53.9 5.8 %collective-permute-start.9 = (bf16[256,256]{1,0:T(8,128)(2,1)S(1)}, bf16[256,256]{1,0:T(8,128)(2,1)S(1)}, u32[]{:S(2)}, u32[]{:S(2)}) collective-permute-start(bf16[256,256]{1,0:T(8,128)(2,1)S(1)} %bitcast.8), channel_id=1, source_target_pairs={{0,32},{32,64},{64,96},{96,0},{1,33},{33,65},{65,97},{97,1},{2,34}... | collective-permute-start | bytes 393224 | tf_op jit(solution)/shard_map/ppermute | solution.py:230
  55.3 14.3 %collective-permute-start.5 = (bf16[512,256]{1,0:T(8,128)(2,1)S(1)}, bf16[512,256]{1,0:T(8,128)(2,1)S(1)}, u32[]{:S(2)}, u32[]{:S(2)}) collective-permute-start(bf16[512,256]{1,0:T(8,128)(2,1)S(1)} %collective-permute-done.4.refs_0_), channel_id=1, source_target_pairs={{0,2},{1,31},{2,4},{3,1},{4,6},{5,3},{6,8},{7,5},{8,10},{9,7},{10,... | collective-permute-start | bytes 786440 | tf_op jit(solution)/shard_map/ppermute | solution.py:238
  56.6 10.2 %collective-permute-start.10 = (bf16[256,256]{1,0:T(8,128)(2,1)S(1)}, bf16[256,256]{1,0:T(8,128)(2,1)S(1)}, u32[]{:S(2)}, u32[]{:S(2)}) collective-permute-start(bf16[256,256]{1,0:T(8,128)(2,1)S(1)} %bitcast.9), channel_id=1, source_target_pairs={{0,96},{32,0},{64,32},{96,64},{1,97},{33,1},{65,33},{97,65},{2,98}... | collective-permute-start | bytes 393224 | tf_op jit(solution)/shard_map/ppermute | solution.py:230
  59.4 7.6 %collective-permute-start.11 = (bf16[256,256]{1,0:T(8,128)(2,1)S(1)}, bf16[256,256]{1,0:T(8,128)(2,1)S(1)}, u32[]{:S(2)}, u32[]{:S(2)}) collective-permute-start(bf16[256,256]{1,0:T(8,128)(2,1)S(1)} %bitcast.10), channel_id=1, source_target_pairs={{0,64},{32,96},{64,0},{96,32},{1,65},{33,97},{65,1},{97,33},{2,66}... | collective-permute-start | bytes 393224 | tf_op jit(solution)/shard_map/ppermute | solution.py:230
  59.7 9.9 %collective-permute-start.12 = (bf16[256,256]{1,0:T(8,128)(2,1)S(1)}, bf16[256,256]{1,0:T(8,128)(2,1)S(1)}, u32[]{:S(2)}, u32[]{:S(2)}) collective-permute-start(bf16[256,256]{1,0:T(8,128)(2,1)S(1)} %bitcast.11), channel_id=1, source_target_pairs={{0,1},{1,0},{2,3},{3,2},{4,5},{5,4},{6,7},{7,6},{8,9},{9,8},{10,11... | collective-permute-start | bytes 393224 | tf_op jit(solution)/shard_map/ppermute | solution.py:232
  63.7 9.2 %collective-permute-start.21 = (bf16[512,256]{1,0:T(8,128)(2,1)S(1)}, bf16[512,256]{1,0:T(8,128)(2,1)S(1)}, u32[]{:S(2)}, u32[]{:S(2)}) collective-permute-start(bf16[512,256]{1,0:T(8,128)(2,1)S(1)} %collective-permute-done.20.refs_1_), channel_id=1, source_target_pairs={{0,2},{1,31},{2,4},{3,1},{4,6},{5,3},{6,8},{7,5},{8,10},{9,7},{10,... | collective-permute-start | bytes 786440 | tf_op jit(solution)/shard_map/ppermute | solution.py:239
  66.8 5.9 %collective-permute-start.13 = (bf16[256,256]{1,0:T(8,128)(2,1)S(1)}, bf16[256,256]{1,0:T(8,128)(2,1)S(1)}, u32[]{:S(2)}, u32[]{:S(2)}) collective-permute-start(bf16[256,256]{1,0:T(8,128)(2,1)S(1)} %collective-permute-done.9.refs_1_), channel_id=1, source_target_pairs={{0,1},{1,0},{2,3},{3,2},{4,5},{5,4},{6,7},{7,6},{8,9},{9,8},{10,11... | collective-permute-start | bytes 393224 | tf_op jit(solution)/shard_map/ppermute | solution.py:232
  69.6 12.3 %collective-permute-start.6 = (bf16[512,256]{1,0:T(8,128)(2,1)S(1)}, bf16[512,256]{1,0:T(8,128)(2,1)S(1)}, u32[]{:S(2)}, u32[]{:S(2)}) collective-permute-start(bf16[512,256]{1,0:T(8,128)(2,1)S(1)} %collective-permute-done.5.refs_0_), channel_id=1, source_target_pairs={{0,2},{1,31},{2,4},{3,1},{4,6},{5,3},{6,8},{7,5},{8,10},{9,7},{10,... | collective-permute-start | bytes 786440 | tf_op jit(solution)/shard_map/ppermute | solution.py:238
  72.9 12.4 %collective-permute-start.22 = (bf16[512,256]{1,0:T(8,128)(2,1)S(1)}, bf16[512,256]{1,0:T(8,128)(2,1)S(1)}, u32[]{:S(2)}, u32[]{:S(2)}) collective-permute-start(bf16[512,256]{1,0:T(8,128)(2,1)S(1)} %collective-permute-done.21.refs_1_), channel_id=1, source_target_pairs={{0,2},{1,31},{2,4},{3,1},{4,6},{5,3},{6,8},{7,5},{8,10},{9,7},{10,... | collective-permute-start | bytes 786440 | tf_op jit(solution)/shard_map/ppermute | solution.py:239
  81.9 10.0 %collective-permute-start.7 = (bf16[512,256]{1,0:T(8,128)(2,1)S(1)}, bf16[512,256]{1,0:T(8,128)(2,1)S(1)}, u32[]{:S(2)}, u32[]{:S(2)}) collective-permute-start(bf16[512,256]{1,0:T(8,128)(2,1)S(1)} %collective-permute-done.6.refs_0_), channel_id=1, source_target_pairs={{0,2},{1,31},{2,4},{3,1},{4,6},{5,3},{6,8},{7,5},{8,10},{9,7},{10,... | collective-permute-start | bytes 786440 | tf_op jit(solution)/shard_map/ppermute | solution.py:243
  85.3 10.3 %collective-permute-start.23 = (bf16[512,256]{1,0:T(8,128)(2,1)S(1)}, bf16[512,256]{1,0:T(8,128)(2,1)S(1)}, u32[]{:S(2)}, u32[]{:S(2)}) collective-permute-start(bf16[512,256]{1,0:T(8,128)(2,1)S(1)} %collective-permute-done.22.refs_1_), channel_id=1, source_target_pairs={{0,2},{1,31},{2,4},{3,1},{4,6},{5,3},{6,8},{7,5},{8,10},{9,7},{10,... | collective-permute-start | bytes 786440 | tf_op jit(solution)/shard_map/ppermute | solution.py:239
  92.0 9.6 %collective-permute-start.8 = (bf16[512,256]{1,0:T(8,128)(2,1)S(1)}, bf16[512,256]{1,0:T(8,128)(2,1)S(1)}, u32[]{:S(2)}, u32[]{:S(2)}) collective-permute-start(bf16[512,256]{1,0:T(8,128)(2,1)S(1)} %collective-permute-done.7.refs_0_), channel_id=1, source_target_pairs={{0,1},{1,0},{2,3},{3,2},{4,5},{5,4},{6,7},{7,6},{8,9},{9,8},{10,11... | collective-permute-start | bytes 786440 | tf_op jit(solution)/shard_map/ppermute | solution.py:244
  104.3 6.5 %collective-permute-start.29 = (bf16[272,256]{1,0:T(8,128)(2,1)S(1)}, bf16[272,256]{1,0:T(8,128)(2,1)S(1)}, u32[]{:S(2)}, u32[]{:S(2)}) collective-permute-start(bf16[272,256]{1,0:T(8,128)(2,1)S(1)} %get-tuple-element.57), channel_id=1, source_target_pairs={{0,32},{32,64},{64,96},{96,0},{1,33},{33,65},{65,97},{97,1},{2,34}... | collective-permute-start | bytes 417800 | tf_op jit(solution)/shard_map/ppermute | solution.py:251
  104.8 7.7 %collective-permute-start.30 = (bf16[272,256]{1,0:T(8,128)(2,1)S(1)}, bf16[272,256]{1,0:T(8,128)(2,1)S(1)}, u32[]{:S(2)}, u32[]{:S(2)}) collective-permute-start(bf16[272,256]{1,0:T(8,128)(2,1)S(1)} %get-tuple-element.58), channel_id=1, source_target_pairs={{0,64},{32,96},{64,0},{96,32},{1,65},{33,97},{65,1},{97,33},{2,66}... | collective-permute-start | bytes 417800 | tf_op jit(solution)/shard_map/ppermute | solution.py:251
  (7 other events, 26.8 us)
